TPU v7x, 256 devices: a 8x8x2 block of a 8x8x16 slice. The times are simulated.
256 devices in a mesh: parts: 2 (over z), rows: 128 (over x, y, core).
Axes of the slice: x: 8, y: 8, z: 2, core: 2. Of those that a mesh axis runs over, the one named last changes fastest.
The devices are a block of a 8x8x16 slice.
Arguments:
- pair: bfloat16 [512, 256, 128], P(('parts', 'rows')), parts along dimension 0, may hold values from -16 to 16
- mask: int32 [512], P('parts'), parts along dimension 0, may hold values from 0 to 1, as said below
- w_tri_in: bfloat16 [128, 512], replicated, may hold values from -0.5 to 0.5
- w_tri_gate: bfloat16 [128, 128], replicated, may hold values from -0.5 to 0.5
- w_tri_out: bfloat16 [128, 128], replicated, may hold values from -0.5 to 0.5
- w_qkv: bfloat16 [128, 384], replicated, may hold values from -0.5 to 0.5
- w_att_bias: bfloat16 [128, 4], replicated, may hold values from -80 to 80
- w_att_gate: bfloat16 [128, 128], replicated, may hold values from -0.5 to 0.5
- w_att_out: bfloat16 [128, 128], replicated, may hold values from -0.5 to 0.5
Outputs:
- updated: bfloat16 [512, 256, 128], P(('parts', 'rows')), parts along dimension 0
There are 2 independent parts, one for each index of `parts`. A program takes and returns all parts, laid end to end along the dimension named above; an argument that names none is the same for every part. Nothing has to cross between parts.
Inputs may be any that keep to these rules, and one draw needn't show every extreme that they name: `mask`: 0 on every residue from some L on, with 128 <= L <= 255; before L each residue may be 1 or 0 (unresolved); residue 0 is always 1.
All inputs are finite; a program needn't handle non-finite values.
Results may differ from a plain program's by a relative error of at most 0.012.
Values may be sent and summed in bfloat16 or wider, within the bound.
A program may use at most 64 MiB of HBM per device.

v0:
```python
import jax
import jax.numpy as jnp
from jax import lax
from jax.sharding import Mesh
from jax.sharding import PartitionSpec as P

HEADS = 4
HEAD_DIM = 32
ROWS = ("rows_0", "rows_1", "rows_2")
PARTS_ROWS = ("parts", "rows_0", "rows_1", "rows_2")


EPSILON = 1e-05
MASK_PENALTY = 1000000000.0


def in_one_piece(arrays, axis, split_dim, concat_dim, along):
    both = jnp.concatenate(arrays, axis=along)
    filled, at, finished = (
        lax.all_to_all(both, axis, split_axis=split_dim, concat_axis=concat_dim, tiled=True),
        0,
        [],
    )
    for a in arrays:
        finished.append(lax.slice_in_dim(filled, at, at + a.shape[along], axis=along))
        at += a.shape[along]
    return tuple(finished)


def split_up(shard, dim, peers):
    dims = shard.shape
    tiles = shard.reshape(*dims[:dim], peers, dims[dim] // peers, *dims[dim + 1 :])
    return jnp.moveaxis(tiles, dim, 0)


def joined_along(tiles, dim):
    tiles = jnp.moveaxis(tiles, 0, dim)
    dims = tiles.shape
    return tiles.reshape(*dims[:dim], dims[dim] * dims[dim + 1], *dims[dim + 2 :])


def exchange_in_order(tiles, axes, sequence):
    inside = tiles.shape[1:]
    filled = tiles.reshape(*(lax.axis_size(a) for a in axes), *inside)
    for k in sequence:
        filled = lax.all_to_all(filled, axes[k], k, k, tiled=True)
    return filled.reshape(-1, *inside)


def two_step_exchange(shard, groups, sequence, split_dim, concat_dim):
    peers = lax.axis_size(groups[0]) * lax.axis_size(groups[1])
    tiles = split_up(shard, split_dim, peers)
    return joined_along(exchange_in_order(tiles, groups, sequence), concat_dim)


def normalize(values, along_axis):
    values = values.astype(jnp.float32)
    center = jnp.mean(values, axis=along_axis, keepdims=True)
    shifted = values - center
    spread = jnp.mean(shifted * shifted, axis=along_axis, keepdims=True)
    return shifted * lax.rsqrt(spread + EPSILON)


def attend(queries, key_rows, values, score_bias, key_penalty, score_scale):
    column_count = queries.shape[1]
    heads_here = queries.shape[2]
    block_size = max(1, 4 // heads_here)

    def reorder(tensor):
        return tensor.reshape(
            tensor.shape[0], column_count // block_size, block_size, heads_here, -1
        ).transpose(1, 0, 2, 3, 4)

    def one_block(inputs):
        query_part, key_part, value_part = inputs
        scores = (
            jnp.einsum("kbhd,ibhd->bhki", key_part, query_part, preferred_element_type=jnp.float32)
            * score_scale
        )
        scores = scores + score_bias[None] + key_penalty[None, None, :, None]
        row_peak = jnp.max(scores, axis=2, keepdims=True)
        weights = jnp.exp(scores - row_peak)
        weights = (weights / jnp.sum(weights, axis=2, keepdims=True)).astype(jnp.bfloat16)
        result = jnp.einsum(
            "bhki,kbhd->ibhd", weights, value_part, preferred_element_type=jnp.float32
        )
        return result.astype(jnp.bfloat16)

    outputs = lax.map(one_block, (reorder(queries), reorder(key_rows), reorder(values)))
    return outputs.transpose(1, 0, 2, 3, 4).reshape(queries.shape)


def local(pair, mask, w_tri_in, w_tri_gate, w_tri_out, w_qkv, w_att_bias, w_att_gate, w_att_out):
    row_count = pair.shape[0]
    residues = pair.shape[1]
    devices = lax.axis_size(ROWS)
    first_row = lax.axis_index(ROWS) * row_count
    key_mask = mask.astype(jnp.float32)
    row_mask = lax.dynamic_slice_in_dim(key_mask, first_row, row_count, 0)
    key_penalty = (key_mask - 1.0) * MASK_PENALTY
    normed = normalize(pair, 2).astype(jnp.bfloat16)
    projected = jnp.einsum("rkc,cf->frk", normed, w_tri_in, preferred_element_type=jnp.float32)
    hidden = w_tri_out.shape[0]
    pair_mask = row_mask[:, None] * key_mask[None, :]
    left_side = (
        jax.nn.sigmoid(projected[:hidden]) * projected[hidden : 2 * hidden] * pair_mask
    ).astype(jnp.bfloat16)
    right_side = (
        jax.nn.sigmoid(projected[2 * hidden : 3 * hidden]) * projected[3 * hidden :] * pair_mask
    ).astype(jnp.bfloat16)
    left_cols, right_cols = in_one_piece((left_side, right_side), ROWS, 0, 1, 2)
    product = jnp.einsum(
        "cik,cjk->cij", left_cols, right_cols, preferred_element_type=jnp.float32
    ).astype(jnp.bfloat16)
    triangle_rows = two_step_exchange(product, (("rows_0", "rows_1"), "rows_2"), (1, 0), 1, 0)
    triangle_normed = normalize(triangle_rows, 0).astype(jnp.bfloat16)
    triangle_gate = jax.nn.sigmoid(
        jnp.einsum("rjc,cd->rjd", normed, w_tri_gate, preferred_element_type=jnp.float32)
    )
    triangle_update = jnp.einsum(
        "crj,cd->rjd", triangle_normed, w_tri_out, preferred_element_type=jnp.float32
    )
    middle = lax.optimization_barrier(
        (pair.astype(jnp.float32) + triangle_gate * triangle_update).astype(jnp.bfloat16)
    )
    attention_input = normalize(middle, 2).astype(jnp.bfloat16)
    bias_rows = jnp.einsum(
        "kic,ch->hki", attention_input, w_att_bias, preferred_element_type=jnp.float32
    )
    score_scale = HEAD_DIM ** (-0.5)
    groups = devices // HEADS
    group_width = residues // groups
    projections = jnp.einsum(
        "rgwc,cthd->hgrtwd",
        attention_input.reshape(row_count, groups, group_width, -1),
        w_qkv.reshape(-1, 3, HEADS, HEAD_DIM),
        preferred_element_type=jnp.float32,
    ).astype(jnp.bfloat16)
    outgoing = projections.reshape(devices, row_count, 3, group_width * HEAD_DIM)
    received = lax.all_to_all(outgoing, ROWS, split_axis=0, concat_axis=1, tiled=True)
    bias_copies = jnp.repeat(bias_rows, groups, axis=0)
    head_bias = lax.all_to_all(bias_copies, ROWS, split_axis=0, concat_axis=1, tiled=True)
    pieces = received.reshape(residues, 3, group_width, 1, HEAD_DIM)
    attended = attend(pieces[:, 0], pieces[:, 1], pieces[:, 2], head_bias, key_penalty, score_scale)
    returned = lax.all_to_all(
        attended.reshape(residues, group_width, HEAD_DIM),
        ROWS,
        split_axis=0,
        concat_axis=1,
        tiled=True,
    )
    attention_rows = (
        returned.reshape(row_count, HEADS, groups, group_width, HEAD_DIM)
        .transpose(0, 2, 3, 1, 4)
        .reshape(row_count, residues, HEADS * HEAD_DIM)
    )
    attention_gate = jax.nn.sigmoid(
        jnp.einsum("rjc,cf->rjf", attention_input, w_att_gate, preferred_element_type=jnp.float32)
    )
    gated_output = (attention_gate * attention_rows.astype(jnp.float32)).astype(jnp.bfloat16)
    result = middle.astype(jnp.float32) + jnp.einsum(
        "rjf,fc->rjc", gated_output, w_att_out, preferred_element_type=jnp.float32
    )
    return result.astype(jnp.bfloat16)


def solution(mesh):
    torus = Mesh(
        mesh.devices.reshape(mesh.shape["parts"], 8, 8, 2), ("parts", "rows_0", "rows_1", "rows_2")
    )
    placed = (P(PARTS_ROWS, None, None), P("parts"), P(), P(), P(), P(), P(), P(), P())
    return jax.shard_map(
        local, mesh=torus, in_specs=placed, out_specs=P(PARTS_ROWS, None, None), check_vma=False
    )
```

profile of v0, /device:TPU:513, one launch (start us, length us, event | category | flops | bytes accessed | tf_op | source)
XLA Modules:
  0.0 146.6 jit_solution(16613823558735798350)
XLA Ops:
  0.0 1.1 convert_reduce_fusion.1
  1.1 1.2 fusion.45
  2.2 0.7 convert_element_type.85
  2.9 0.1 dynamic_slice.13
  3.0 0.1 broadcast_multiply_fusion
  3.1 1.2 convolution_bitcast_fusion
  4.3 0.2 fusion.53
  4.5 0.0 copy-start.1
  4.5 0.0 copy-start.8
  4.6 0.2 copy.40
  4.7 41.2 %all_to_all.55 = bf16[128,2,512]{2,1,0:T(2,128)(2,1)S(1)} all-to-all(bf16[128,2,512]{2,1,0:T(2,128)(2,1)S(1)} %copy.40), channel_id=1, replica_groups=mesh['parts'=2,'rows_0'=8,'rows_1'=8,'rows_2'=2] {'rows_0','rows_1','row..., dimensions={0} | all-to-all | bytes 524288 | tf_op jit(solution)/shard_map/all_to_all | solution.py:20
  45.9 0.1 all_to_all.19
  46.0 0.2 convolution_convert_fusion.2
  46.2 0.0 copy-start.6
  46.2 0.1 reshape_transpose_reshape.3
  46.3 0.1 copy.41
  46.4 4.2 %all_to_all.56 = bf16[64,2,1,2,256]{4,3,0,2,1:T(2,128)(2,1)S(1)} all-to-all(bf16[64,2,1,2,256]{4,3,0,2,1:T(2,128)(2,1)S(1)} %copy.41), channel_id=1, replica_groups=mesh['parts'=2,'rows_0'=8,'rows_1'=8,'rows_2'=2] {'rows_2'}, dimensions={1} | all-to-all | bytes 262144 | tf_op jit(solution)/shard_map/all_to_all | solution.py:46
  50.6 0.7 copy.42
  51.4 6.6 %all-to-all-start.2 = ((bf16[64,2,1,2,256]{4,3,1,2,0:T(2,128)(2,1)}), bf16[64,2,1,2,256]{4,3,1,2,0:T(2,128)(2,1)S(1)}, u32[]{:S(2)}, u32[]{:S(2)}) async-start(bf16[64,2,1,2,256]{4,3,1,2,0:T(2,128)(2,1)} %copy.42), calls=%async_computation.2 | async-start | bytes 262144 | tf_op jit(solution)/shard_map/all_to_all | solution.py:46
  58.0 0.3 fusion.35
  58.3 0.0 copy-start.5
  58.3 9.9 %all-to-all-done.2 = bf16[64,2,1,2,256]{4,3,1,2,0:T(2,128)(2,1)S(1)} async-done(((bf16[64,2,1,2,256]{4,3,1,2,0:T(2,128)(2,1)}), bf16[64,2,1,2,256]{4,3,1,2,0:T(2,128)(2,1)S(1)}, u32[]{:S(2)}, u32[]{:S(2)}) %all-to-all-start.2) | async-done | bytes 131104 | tf_op jit(solution)/shard_map/all_to_all | solution.py:46
  68.2 0.2 convert_reduce_fusion.2
  68.4 0.2 multiply_reduce_fusion
  68.6 0.1 fusion.58
  68.8 0.2 fusion.37
  69.0 0.1 convert_reduce_fusion
  69.1 0.3 fusion.43
  69.4 0.3 convolution_bitcast_fusion.1
  69.7 0.8 broadcast_in_dim.8
  70.5 9.1 %all-to-all-start.4 = ((f32[128,2,256]{2,1,0:T(2,128)}), f32[128,2,256]{2,1,0:T(2,128)S(1)}, u32[]{:S(2)}, u32[]{:S(2)}) async-start(f32[128,2,256]{2,1,0:T(2,128)} %bitcast.30), calls=%async_computation.4 | async-start | bytes 524288 | tf_op jit(solution)/shard_map/all_to_all | solution.py:142
  79.7 0.1 copy.44
  79.8 0.6 fusion.27
  80.4 0.3 copy.57
  80.7 0.0 copy-start.7
  80.7 1.7 %reshape.165 = bf16[128,2,3,256]{3,1,2,0:T(2,128)(2,1)} reshape(bf16[4,32,2,3,8,32]{5,4,2,3,1,0:T(8,128)(2,1)S(1)} %copy.57) | data formatting | bytes 786432 | tf_op jit(solution)/shard_map/reshape | solution.py:139
  82.4 11.6 %all-to-all-done.4 = f32[128,2,256]{2,1,0:T(2,128)S(1)} async-done(((f32[128,2,256]{2,1,0:T(2,128)}), f32[128,2,256]{2,1,0:T(2,128)S(1)}, u32[]{:S(2)}, u32[]{:S(2)}) %all-to-all-start.4) | async-done | bytes 262176 | tf_op jit(solution)/shard_map/all_to_all | solution.py:142
  94.0 7.7 %all-to-all-start.3 = ((bf16[128,2,3,256]{3,1,2,0:T(2,128)(2,1)}), bf16[128,2,3,256]{3,1,2,0:T(2,128)(2,1)S(1)}, u32[]{:S(2)}, u32[]{:S(2)}) async-start(bf16[128,2,3,256]{3,1,2,0:T(2,128)(2,1)} %reshape.165), calls=%async_computation.3 | async-start | bytes 786432 | tf_op jit(solution)/shard_map/all_to_all | solution.py:140
  101.8 0.2 all_to_all.46
  102.0 16.5 %all-to-all-done.3 = bf16[128,2,3,256]{3,1,2,0:T(2,128)(2,1)S(1)} async-done(((bf16[128,2,3,256]{3,1,2,0:T(2,128)(2,1)}), bf16[128,2,3,256]{3,1,2,0:T(2,128)(2,1)S(1)}, u32[]{:S(2)}, u32[]{:S(2)}) %all-to-all-start.3) | async-done | bytes 393248 | tf_op jit(solution)/shard_map/all_to_all | solution.py:140
  118.5 0.3 copy.47
  118.7 0.7 reshape.151
  119.5 0.1 fusion.89
  119.6 0.0 copy-start.4
  119.6 0.3 copy.48
  119.9 0.3 copy.49
  120.2 0.3 copy.50
  120.6 2.5 %while.10 = (s32[]{:T(128)}, bf16[2,256,4,1,32]{1,4,2,3,0:T(8,128)(2,1)S(1)}, bf16[2,256,4,1,32]{1,4,2,3,0:T(8,128)(2,1)S(1)}, bf16[2,256,4,1,32]{1,4,2,3,0:T(8,...) while((s32[]{:T(128)}, ...), condition=%wide.region_9.10_spmd, body=%wide.region_6.9_spmd.sunk | while | flops 53249536 | bytes 4076637 | solution.py:89
  120.6 0.5 fusion.107
  121.1 0.3 fusion.108
  121.5 0.3 fusion.109
  121.8 0.5 fusion.107
  122.4 0.3 fusion.108
  122.7 0.3 fusion.109
  123.1 0.3 copy.52
  123.4 0.3 reshape.166
  123.7 20.2 %all_to_all.57 = bf16[128,2,256]{2,1,0:T(2,128)(2,1)S(1)} all-to-all(bf16[128,2,256]{2,1,0:T(2,128)(2,1)S(1)} %reshape.166), channel_id=1, replica_groups=mesh['parts'=2,'rows_0'=8,'rows_1'=8,'rows_2'=2] {'rows_0','rows_1','row..., dimensions={0} | all-to-all | bytes 262144 | tf_op jit(solution)/shard_map/all_to_all | solution.py:145
  143.9 0.3 reshape.167
  144.2 0.1 convert.5
  144.3 0.0 copy-start.9
  144.3 0.0 copy-start.10
  144.3 0.7 copy.64
  145.0 0.5 reshape.154
  145.5 1.1 fusion.38
  (26 shorter events, 0.1 us)
Async XLA Ops:
  0.0 3.1 %copy-start = (bf16[128,512]{1,0:T(8,128)(2,1)S(1)}, bf16[128,512]{1,0:T(8,128)(2,1)}, u32[]{:S(2)}) copy-start(bf16[128,512]{1,0:T(8,128)(2,1)} %param.13) | copy-start | bytes 393220
  4.5 53.4 %copy-start.1 = (bf16[2,256,128]{2,1,0:T(8,128)(2,1)S(1)}, bf16[2,256,128]{2,1,0:T(8,128)(2,1)}, u32[]{:S(2)}) copy-start(bf16[2,256,128]{2,1,0:T(8,128)(2,1)} %param.11) | copy-start | bytes 393220
  4.5 53.4 %copy-start.8 = (bf16[128,128]{1,0:T(8,128)(2,1)S(1)}, bf16[128,128]{1,0:T(8,128)(2,1)}, u32[]{:S(2)}) copy-start(bf16[128,128]{1,0:T(8,128)(2,1)} %param.14) | copy-start | bytes 98308
  46.2 22.5 %copy-start.6 = (bf16[128,128]{1,0:T(8,128)(2,1)S(1)}, bf16[128,128]{1,0:T(8,128)(2,1)}, u32[]{:S(2)}) copy-start(bf16[128,128]{1,0:T(8,128)(2,1)} %param.15) | copy-start | bytes 98308
  51.4 18.0 %copy-start.11 = (bf16[128,4]{0,1:T(4,128)(2,1)S(1)}, bf16[128,4]{0,1:T(4,128)(2,1)}, u32[]{:S(2)}) copy-start(bf16[128,4]{0,1:T(4,128)(2,1)} %param.17) | copy-start | bytes 3076
  51.4 16.8 %all-to-all-start.2 = ((bf16[64,2,1,2,256]{4,3,1,2,0:T(2,128)(2,1)}), bf16[64,2,1,2,256]{4,3,1,2,0:T(2,128)(2,1)S(1)}, u32[]{:S(2)}, u32[]{:S(2)}) async-start(bf16[64,2,1,2,256]{4,3,1,2,0:T(2,128)(2,1)} %copy.42), calls=%async_computation.2 | async-start | bytes 262144 | tf_op jit(solution)/shard_map/all_to_all | solution.py:46
  58.3 21.3 %copy-start.5 = (bf16[128,384]{1,0:T(8,128)(2,1)S(1)}, bf16[128,384]{1,0:T(8,128)(2,1)}, u32[]{:S(2)}) copy-start(bf16[128,384]{1,0:T(8,128)(2,1)} %param.16) | copy-start | bytes 294916
  69.0 10.8 %copy-start.2 = (bf16[2,256,128]{2,1,0:T(8,128)(2,1)}, bf16[2,256,128]{2,1,0:T(8,128)(2,1)S(1)}, u32[]{:S(2)}) copy-start(bf16[2,256,128]{2,1,0:T(8,128)(2,1)S(1)} %fusion.37) | copy-start | bytes 393220
  70.5 23.5 %all-to-all-start.4 = ((f32[128,2,256]{2,1,0:T(2,128)}), f32[128,2,256]{2,1,0:T(2,128)S(1)}, u32[]{:S(2)}, u32[]{:S(2)}) async-start(f32[128,2,256]{2,1,0:T(2,128)} %bitcast.30), calls=%async_computation.4 | async-start | bytes 524288 | tf_op jit(solution)/shard_map/all_to_all | solution.py:142
  80.7 21.0 %copy-start.7 = (s32[256]{0:T(256)S(1)}, s32[256]{0:T(256)}, u32[]{:S(2)}) copy-start(s32[256]{0:T(256)} %param.12) | copy-start | bytes 3076
  94.0 24.4 %all-to-all-start.3 = ((bf16[128,2,3,256]{3,1,2,0:T(2,128)(2,1)}), bf16[128,2,3,256]{3,1,2,0:T(2,128)(2,1)S(1)}, u32[]{:S(2)}, u32[]{:S(2)}) async-start(bf16[128,2,3,256]{3,1,2,0:T(2,128)(2,1)} %reshape.165), calls=%async_computation.3 | async-start | bytes 786432 | tf_op jit(solution)/shard_map/all_to_all | solution.py:140
  119.6 1.0 copy-start.4
  144.3 1.2 copy-start.3
  144.3 1.2 copy-start.9
  144.3 1.2 copy-start.10
where the time goes:
time: 147 us
  blocking collectives  65.5 us (45%)
  waiting for transfers between devices  37.9 us (26%)
  starting transfers between devices  23.5 us (16%)
  local copies, waits for them, and re-layouts  8.56 us (6%)
  matrix products  6.53 us (4%)
  other arithmetic  4.18 us (3%)
    all_to_all x1, blocking collectives, in_one_piece(): lax.all_to_all(both, axis, split_axis=split_dim, concat_axis=concat_dim,...  41.2 us
    all_to_all x1, blocking collectives, local(): lax.all_to_all(attended.reshape(residues, group_width, HEAD_DIM), ROWS, s...  20.2 us
    all_to_all x1, waiting for transfers between devices, local(): lax.all_to_all(outgoing, ROWS, split_axis=0, concat_axis=1, tiled=True)  16.5 us
    all_to_all x1, waiting for transfers between devices, local(): lax.all_to_all(bias_copies, ROWS, split_axis=0, concat_axis=1, tiled=True)  11.6 us
    all_to_all x1, waiting for transfers between devices, exchange_in_order(): filled = lax.all_to_all(filled, axes[k], k, k, tiled=True)  9.86 us
    all_to_all x1, starting transfers between devices, local(): lax.all_to_all(bias_copies, ROWS, split_axis=0, concat_axis=1, tiled=True)  9.14 us
    all_to_all x1, starting transfers between devices, local(): lax.all_to_all(outgoing, ROWS, split_axis=0, concat_axis=1, tiled=True)  7.7 us
    all_to_all x1, starting transfers between devices, exchange_in_order(): filled = lax.all_to_all(filled, axes[k], k, k, tiled=True)  6.61 us
  transfers between devices with their start and end apart: 3, of which 3 were waited for; matrix products, arithmetic and copies ran while one was open for 2% of the time, Pallas kernels for 0%

commit v1 on v0

v1 whole, which is shorter than its diff:
```python
import functools

import jax
import jax.numpy as jnp
from jax import lax
from jax.experimental import pallas as pl
from jax.experimental.pallas import tpu as pltpu
from jax.sharding import PartitionSpec as P

HEADS = 4
HEAD_DIM = 32
EPSILON = 1e-05
MASK_PENALTY = 1000000000.0
MESH = pl.DeviceIdType.MESH
BF = jnp.bfloat16
F32 = jnp.float32
NN = (((1,), (0,)), ((), ()))
NT = (((1,), (1,)), ((), ()))
TN = (((0,), (0,)), ((), ()))


def dot(a, b, dims=NN):
    return lax.dot_general(a, b, dims, preferred_element_type=F32)


def sigmoid(x):
    return 0.5 * jnp.tanh(0.5 * x) + 0.5


def norm_lanes(x):
    center = jnp.mean(x, axis=1, keepdims=True)
    shifted = x - center
    spread = jnp.mean(shifted * shifted, axis=1, keepdims=True)
    return shifted * lax.rsqrt(spread + EPSILON)


def iota(shape, dim):
    return lax.broadcasted_iota(jnp.int32, shape, dim)


def spread_rows(rows, picked, parity):
    return (iota((rows, picked), 0) == 2 * iota((rows, picked), 1) + parity).astype(F32).astype(BF)


def whole_wait(ref, sem):
    pltpu.make_async_copy(ref, ref, sem).wait()


def kernel(
    n,
    pair_ref, mask_ref, w_in_ref, w_tg_ref, w_to_ref, w_qkv_ref, w_ab_ref, w_ag_ref, w_ao_ref,
    out_ref,
    pair_send, edge_send, edge_recv, pair_recv, prod_send, prod_recv, tokens, middle, att_own, att_peer,
    bias_send, bias_recv, scores, o_send, o_recv, o_own, upd_send, upd_recv,
    send_sem, recv_sem,
):
    rows, res, cz = pair_ref.shape
    me = lax.axis_index("rows")
    core = lax.rem(me, 2)
    partner = me + 1 - 2 * core

    barrier = pltpu.get_barrier_semaphore()

    def peer(t):
        return lax.rem(me + t, n)

    def greet(t, carry):
        pl.semaphore_signal(barrier, inc=1, device_id={"rows": peer(t)}, device_id_type=MESH)
        return carry

    lax.fori_loop(1, n, greet, 0)

    def exchange(source, target, k):
        def send(t, carry):
            d = peer(t)
            pltpu.make_async_remote_copy(
                src_ref=source(d), dst_ref=target, send_sem=send_sem.at[k], recv_sem=recv_sem.at[k],
                device_id={"rows": d}, device_id_type=MESH,
            ).start()
            return carry

        lax.fori_loop(1, n, send, 0)
        pltpu.make_async_copy(source(me), target, recv_sem.at[k]).start()

    def to_partner(source, target, k):
        copy = pltpu.make_async_remote_copy(
            src_ref=source, dst_ref=target, send_sem=send_sem.at[k], recv_sem=recv_sem.at[k],
            device_id={"rows": partner}, device_id_type=MESH,
        )
        copy.start()
        return copy

    key_mask = mask_ref[...].astype(F32)
    lane = iota((1, res), 1)
    row_mask = [
        jnp.sum(jnp.where(lane == me * rows + r, key_mask, 0.0), axis=1, keepdims=True) for r in range(rows)
    ]
    spreads = [spread_rows(2 * cz, cz, r) for r in range(2)]
    pair_send[...] = pair_ref[...].reshape(rows, n, 2, cz)
    normed = jnp.concatenate(
        [norm_lanes(pair_ref[r].astype(F32)).astype(BF) for r in range(rows)], axis=1
    )

    def projected(g):
        w = w_in_ref[:, g * cz : (g + 1) * cz]
        spread_w = jnp.concatenate([dot(s, w, NT).astype(BF) for s in spreads], axis=1)
        return dot(spread_w, normed, NT)

    parity = iota((2 * cz, res), 0) % 2
    pair_mask = jnp.where(parity == 0, row_mask[0], row_mask[1]) * key_mask
    for a in range(2):
        edge = (sigmoid(projected(2 * a)) * projected(2 * a + 1) * pair_mask).astype(BF)
        edge_send[:, a] = edge.reshape(n, 2, res)

    pl.semaphore_wait(barrier, n - 1)
    exchange(lambda d: edge_send.at[d], edge_recv.at[me], 0)
    exchange(lambda d: pair_send.at[:, d], pair_recv.at[me], 1)

    whole_wait(edge_recv, recv_sem.at[0])
    left = edge_recv[:, 0].reshape(res, res)
    right = edge_recv[:, 1].reshape(res, res)
    prod_send[...] = dot(right, left, NT).astype(BF).reshape(n, 2, res)
    exchange(lambda d: prod_send.at[d], prod_recv.at[me], 2)

    whole_wait(pair_recv, recv_sem.at[1])
    tokens[...] = pair_recv[...].reshape(2 * res, cz).astype(F32)
    columns = [tokens[pl.ds(jj, res, stride=2), :] for jj in range(2)]
    gates = [sigmoid(dot(norm_lanes(x).astype(BF), w_tg_ref[...])) for x in columns]
    w_to = w_to_ref[...]
    spread_out = jnp.concatenate([dot(s, w_to).astype(BF) for s in spreads], axis=1)
    e_row = iota((8, HEADS), 0)
    e_col = iota((8, HEADS), 1)
    w_bias = jnp.concatenate(
        [
            dot(((e_row // 2 == e_col) & (e_row % 2 == jj)).astype(F32).astype(BF), w_ab_ref[...], NT).astype(BF)
            for jj in range(2)
        ],
        axis=1,
    )

    whole_wait(prod_recv, recv_sem.at[2])
    product = prod_recv[...].reshape(2 * cz, res).astype(F32)
    sub = iota((8, res), 0) % 2

    def column_mean(x):
        total = jnp.sum(x.reshape(2 * cz // 8, 8, res), axis=0)
        even = jnp.sum(jnp.where(sub == 0, total, 0.0), axis=0, keepdims=True)
        odd = jnp.sum(jnp.where(sub == 0, 0.0, total), axis=0, keepdims=True)
        return jnp.where(sub == 0, even, odd) * (1.0 / cz)

    tall = product.reshape(2 * cz // 8, 8, res)
    tall = tall - column_mean(product)[None]
    spread = column_mean((tall * tall).reshape(2 * cz, res))
    tri = (tall * lax.rsqrt(spread + EPSILON)[None]).reshape(2 * cz, res).astype(BF)
    update = dot(tri, spread_out, TN)
    for jj in range(2):
        mid = (columns[jj] + gates[jj] * update[:, jj * cz : (jj + 1) * cz]).astype(BF).astype(F32)
        middle[jj] = mid
        att_own[jj] = norm_lanes(mid).astype(BF)
    to_partner(att_own, att_peer, 4)
    both = jnp.concatenate([att_own[0], att_own[1]], axis=1)
    bias_send[...] = dot(w_bias, both, NT).reshape(2, 4, res)
    exchange(lambda d: bias_send.at[lax.rem(d, 2)], bias_recv.at[me], 3)

    penalty = (key_mask - 1.0) * MASK_PENALTY
    lane_head = iota((1, cz), 1) // HEAD_DIM
    head_mask = [lane_head == 2 * core + h for h in range(2)]
    values = []
    for l in range(4):
        if l == 2:
            whole_wait(att_peer, recv_sem.at[4])
        x = att_own[l] if l < 2 else att_peer[l - 2]
        qkv = dot(x, w_qkv_ref[...]).astype(BF)
        for h in range(2):
            key = jnp.where(head_mask[h], qkv[:, cz : 2 * cz], 0)
            scores[2 * l + h] = dot(qkv[:, :cz], key, NT) * (HEAD_DIM ** -0.5) + penalty
        values.append(qkv[:, 2 * cz :])
    att_gates = [sigmoid(dot(att_own[jj], w_ag_ref[...])) for jj in range(2)]

    whole_wait(bias_recv, recv_sem.at[3])
    any_head = head_mask[0] | head_mask[1]

    def attended(l):
        total = None
        for h in range(2):
            s = scores[2 * l + h] + bias_recv[:, 2 * h : 2 * h + 2].reshape(res, res)
            e = jnp.exp(s - jnp.max(s, axis=1, keepdims=True)).astype(BF)
            ones = jnp.broadcast_to(jnp.where(head_mask[h], 1.0, 0.0), (res, cz)).astype(BF)
            part = dot(e, jnp.concatenate([jnp.where(head_mask[h], values[l], 0), ones], axis=1))
            total = part if total is None else total + part
        return (total[:, :cz] / jnp.where(any_head, total[:, cz:], 1.0)).astype(BF)

    for l in (2, 3):
        o_send[l - 2] = attended(l)
        to_partner(o_send.at[l - 2], o_recv.at[l - 2], 3 + l)
    for jj in range(2):
        o_own[jj] = attended(jj)
    for jj in range(2):
        whole_wait(o_recv.at[jj], recv_sem.at[5 + jj])
        att = o_own[jj].astype(F32) + o_recv[jj].astype(F32)
        gated = (att_gates[jj] * att).astype(BF)
        tokens[pl.ds(jj, res, stride=2), :] = middle[jj] + dot(gated, w_ao_ref[...])
    upd_send[...] = tokens[...].astype(BF).reshape(n, rows, 2, cz)
    exchange(lambda d: upd_send.at[d], upd_recv.at[:, me], 7)
    whole_wait(upd_recv, recv_sem.at[7])
    out_ref[...] = upd_recv[...].reshape(rows, res, cz)

    others = pl.ds(0, n - 1)
    whole_wait(edge_recv.at[others], send_sem.at[0])
    whole_wait(pair_recv.at[others], send_sem.at[1])
    whole_wait(prod_recv.at[others], send_sem.at[2])
    whole_wait(bias_recv.at[others], send_sem.at[3])
    whole_wait(att_peer, send_sem.at[4])
    whole_wait(o_recv.at[0], send_sem.at[5])
    whole_wait(o_recv.at[1], send_sem.at[6])
    whole_wait(upd_recv.at[:, others], send_sem.at[7])


def local(n, pair, mask, w_tri_in, w_tri_gate, w_tri_out, w_qkv, w_att_bias, w_att_gate, w_att_out):
    rows, res, cz = pair.shape
    vmem = pl.BlockSpec(memory_space=pltpu.VMEM)
    return pl.pallas_call(
        functools.partial(kernel, n),
        out_shape=jax.ShapeDtypeStruct(pair.shape, BF),
        in_specs=[vmem] * 9,
        out_specs=vmem,
        scratch_shapes=[
            pltpu.VMEM((rows, n, 2, cz), BF),
            pltpu.VMEM((n, 2, 2, res), BF),
            pltpu.VMEM((n, 2, 2, res), BF),
            pltpu.VMEM((n, rows, 2, cz), BF),
            pltpu.VMEM((n, 2, res), BF),
            pltpu.VMEM((n, 2, res), BF),
            pltpu.VMEM((2 * res, cz), F32),
            pltpu.VMEM((2, res, cz), F32),
            pltpu.VMEM((2, res, cz), BF),
            pltpu.VMEM((2, res, cz), BF),
            pltpu.VMEM((2, 4, res), F32),
            pltpu.VMEM((n, 4, res), F32),
            pltpu.VMEM((8, res, res), F32),
            pltpu.VMEM((2, res, cz), BF),
            pltpu.VMEM((2, res, cz), BF),
            pltpu.VMEM((2, res, cz), BF),
            pltpu.VMEM((n, rows, 2, cz), BF),
            pltpu.VMEM((rows, n, 2, cz), BF),
            pltpu.SemaphoreType.DMA((8,)),
            pltpu.SemaphoreType.DMA((8,)),
        ],
        compiler_params=pltpu.CompilerParams(collective_id=0, has_side_effects=True),
        name="pair_update",
    )(pair, mask.reshape(1, res), w_tri_in, w_tri_gate, w_tri_out, w_qkv, w_att_bias, w_att_gate, w_att_out)


def solution(mesh):
    split = P(("parts", "rows"), None, None)
    placed = (split, P("parts"), P(), P(), P(), P(), P(), P(), P())
    return jax.shard_map(
        functools.partial(local, mesh.shape["rows"]), mesh=mesh, in_specs=placed, out_specs=split, check_vma=False
    )
```

time: 147 us -> 81.8 us (0.56)
  Pallas kernels: 0 us -> 78.7 us
  blocking collectives: 65.5 us -> 0 us
  waiting for transfers between devices: 37.9 us -> 0 us
  starting transfers between devices: 23.5 us -> 0 us
  matrix products: 6.53 us -> 0 us
  local copies, waits for them, and re-layouts: 8.56 us -> 2.98 us
  other arithmetic: 4.18 us -> 0 us
    pallas_call x0 -> x1, Pallas kernels: none -> 78.7 us  [local(): pl.pallas_call(functools.partial(kernel, n), out_shape=jax.ShapeDtypeStru...]
    all_to_all x3 -> x0, blocking collectives: 65.5 us -> none  [the longest x1 41.2 us: in_one_piece(): lax.all_to_all(both, axis, split_axis=split_dim, concat_axis=concat_dim,...]
    all_to_all x3 -> x0, waiting for transfers between devices: 37.9 us -> none  [the longest x1 16.5 us: local(): lax.all_to_all(outgoing, ROWS, split_axis=0, concat_axis=1, tiled=True)]
    all_to_all x3 -> x0, starting transfers between devices: 23.5 us -> none  [the longest x1 9.14 us: local(): lax.all_to_all(bias_copies, ROWS, split_axis=0, concat_axis=1, tiled=True)]
    dot_general x11 -> x0, matrix products: 5.46 us -> none  [the longest x1 1.25 us: local(): jnp.einsum('rkc,cf->frk', normed, w_tri_in, preferred_element_type=jnp.fl...]
    reduce_sum x6 -> x0, other arithmetic: 2.96 us -> none  [the longest x3 1.63 us: normalize(): spread = jnp.mean(shifted * shifted, axis=along_axis, keepdims=True)]
    reshape x3 -> x0, local copies, waits for them, and re-layouts: 2.74 us -> none  [the longest x2 2 us: local(): projections.reshape(devices, row_count, 3, group_width * HEAD_DIM)]
    unnamed x27 -> x4, local copies, waits for them, and re-layouts: 0.8 us -> 2.98 us
  transfers between devices with their start and end apart: 3 -> 0, of which waited for: 3 -> 0; matrix products, arithmetic and copies ran while one was open for 2% -> 0% of each run, Pallas kernels for 0% -> 0%
where the time goes in v1:
time: 81.8 us; the launch traced here: 81.7 us
  Pallas kernels  78.7 us (96%)
  local copies, waits for them, and re-layouts  2.98 us (4%)
    pallas_call x1, Pallas kernels, local(): pl.pallas_call(functools.partial(kernel, n), out_shape=jax.ShapeDtypeStru...  78.7 us
    unnamed x4, local copies, waits for them, and re-layouts  2.98 us

profile of v1, /device:TPU:513, one launch (start us, length us, event | category | flops | bytes accessed | tf_op | source)
XLA Modules:
  0.0 81.7 jit_solution(7194268189463225649)
XLA Ops:
  0.0 0.0 copy-start
  0.0 0.7 copy-done
  0.7 0.7 copy.10.w_ab_ref
  1.4 78.7 %pair_update.1 = bf16[2,256,128]{2,1,0:T(8,128)(2,1)} custom-call(bf16[2,256,128]{2,1,0:T(8,128)(2,1)} %pair_ref.1, s32[1,256]{1,0:T(1,128)} %bitcast.1, bf16[128,512]{1,0:T(8,128)(2,1)} %w_in_ref.1, bf16[128,128]{1,0:T(8,128)(2,1)} %w_tg_ref.1, bf16[128,128]{1,0:T(8,128)(2,1)} %w_to_ref.1, bf16[128,384]{1,0:T(8,128)(2,1)} %w_qkv_ref.1, ...), custom_call_target="tpu_custom_call" | custom-call | tf_op jit(solution)/shard_map/pair_update/pallas_call | solution.py:222
  80.1 1.6 %copy.12 = bf16[2,256,128]{2,1,0:T(8,128)(2,1)} copy(bf16[2,256,128]{2,1,0:T(8,128)(2,1)} %pair_update.1) | data formatting | bytes 262144
Async XLA Ops:
  0.0 0.7 copy-start

commit v2 on v1

--- a/solution.py
+++ b/solution.py
@@ -17,6 +17,17 @@
 NN = (((1,), (0,)), ((), ()))
 NT = (((1,), (1,)), ((), ()))
 TN = (((0,), (0,)), ((), ()))
+
+import random
+
+
+def far_first():
+    order = [(x, y, c) for x in range(8) for y in range(8) for c in range(2) if x + y + c]
+    random.Random(1).shuffle(order)
+    return sorted(order, key=lambda o: -(min(o[0], 8 - o[0]) + min(o[1], 8 - o[1])))
+
+
+ORDER = far_first()
 
 
 def dot(a, b, dims=NN):
@@ -71,15 +82,12 @@
     lax.fori_loop(1, n, greet, 0)
 
     def exchange(source, target, k):
-        def send(t, carry):
-            d = peer(t)
+        for tx, ty, tc in ORDER:
+            d = (((me // 16 + tx) % 8) * 8 + (me // 2 + ty) % 8) * 2 + (core + tc) % 2
             pltpu.make_async_remote_copy(
                 src_ref=source(d), dst_ref=target, send_sem=send_sem.at[k], recv_sem=recv_sem.at[k],
                 device_id={"rows": d}, device_id_type=MESH,
             ).start()
-            return carry
-
-        lax.fori_loop(1, n, send, 0)
         pltpu.make_async_copy(source(me), target, recv_sem.at[k]).start()
 
     def to_partner(source, target, k):

time: 81.8 us -> 75 us (0.917)
  Pallas kernels: 78.7 us -> 71.9 us
    pallas_call x1, Pallas kernels: 78.7 us -> 71.9 us  [local(): pl.pallas_call(functools.partial(kernel, n), out_shape=jax.ShapeDtypeStru...]
where the time goes in v2:
time: 75 us; the launch traced here: 74.9 us
  Pallas kernels  71.9 us (96%)
  local copies, waits for them, and re-layouts  2.98 us (4%)
    pallas_call x1, Pallas kernels, local(): pl.pallas_call(functools.partial(kernel, n), out_shape=jax.ShapeDtypeStru...  71.9 us
    unnamed x4, local copies, waits for them, and re-layouts  2.98 us

profile of v2, /device:TPU:513, one launch (start us, length us, event | category | flops | bytes accessed | tf_op | source)
XLA Modules:
  0.0 74.9 jit_solution(2499016022946711962)
XLA Ops:
  0.0 0.0 copy-start
  0.0 0.7 copy-done
  0.7 0.7 copy.10.w_ab_ref
  1.4 71.9 %pair_update.1 = bf16[2,256,128]{2,1,0:T(8,128)(2,1)} custom-call(bf16[2,256,128]{2,1,0:T(8,128)(2,1)} %pair_ref.1, s32[1,256]{1,0:T(1,128)} %bitcast.1, bf16[128,512]{1,0:T(8,128)(2,1)} %w_in_ref.1, bf16[128,128]{1,0:T(8,128)(2,1)} %w_tg_ref.1, bf16[128,128]{1,0:T(8,128)(2,1)} %w_to_ref.1, bf16[128,384]{1,0:T(8,128)(2,1)} %w_qkv_ref.1, ...), custom_call_target="tpu_custom_call" | custom-call | tf_op jit(solution)/shard_map/pair_update/pallas_call | solution.py:230
  73.3 1.6 %copy.12 = bf16[2,256,128]{2,1,0:T(8,128)(2,1)} copy(bf16[2,256,128]{2,1,0:T(8,128)(2,1)} %pair_update.1) | data formatting | bytes 262144
Async XLA Ops:
  0.0 0.7 copy-start

commit v3 on v1

--- a/solution.py
+++ b/solution.py
@@ -1,4 +1,6 @@
 import functools
+import math
+import random
 
 import jax
 import jax.numpy as jnp
@@ -18,14 +20,16 @@
 NT = (((1,), (1,)), ((), ()))
 TN = (((0,), (0,)), ((), ()))
 
+def far_first(side):
+    order = [(x, y, c) for x in range(side) for y in range(side) for c in range(2) if x + y + c]
+    random.Random(1).shuffle(order)
+    return sorted(order, key=lambda o: -(min(o[0], side - o[0]) + min(o[1], side - o[1])))
 
 def dot(a, b, dims=NN):
     return lax.dot_general(a, b, dims, preferred_element_type=F32)
 
-
 def sigmoid(x):
     return 0.5 * jnp.tanh(0.5 * x) + 0.5
-
 
 def norm_lanes(x):
     center = jnp.mean(x, axis=1, keepdims=True)
@@ -33,62 +37,115 @@
     spread = jnp.mean(shifted * shifted, axis=1, keepdims=True)
     return shifted * lax.rsqrt(spread + EPSILON)
 
-
 def iota(shape, dim):
     return lax.broadcasted_iota(jnp.int32, shape, dim)
 
-
 def spread_rows(rows, picked, parity):
     return (iota((rows, picked), 0) == 2 * iota((rows, picked), 1) + parity).astype(F32).astype(BF)
 
-
 def whole_wait(ref, sem):
     pltpu.make_async_copy(ref, ref, sem).wait()
 
-
 def kernel(
     n,
+    pair_hbm, mask_hbm, w_in_hbm, w_tg_hbm, w_to_hbm, w_qkv_hbm, w_ab_hbm, w_ag_hbm, w_ao_hbm,
+    out_ref,
     pair_ref, mask_ref, w_in_ref, w_tg_ref, w_to_ref, w_qkv_ref, w_ab_ref, w_ag_ref, w_ao_ref,
-    out_ref,
-    pair_send, edge_send, edge_recv, pair_recv, prod_send, prod_recv, tokens, middle, att_own, att_peer,
-    bias_send, bias_recv, scores, o_send, o_recv, o_own, upd_send, upd_recv,
-    send_sem, recv_sem,
+    pair_send, pair_mid, pair_recv, edge_send, edge_mid, edge_recv, prod_send, prod_recv,
+    tokens, middle, att_own, att_peer, bias_send, bias_recv, scores, o_send, o_recv, o_own, upd_send, upd_recv,
+    load_sem, send_sem, recv_sem, edge_sem, pair_sem, bias_sem,
 ):
+    loads = [
+        pltpu.make_async_copy(hbm, ref, load_sem.at[i])
+        for i, (hbm, ref) in enumerate(
+            zip(
+                (pair_hbm, mask_hbm, w_in_hbm, w_tg_hbm, w_to_hbm, w_qkv_hbm, w_ab_hbm, w_ag_hbm, w_ao_hbm),
+                (pair_ref, mask_ref, w_in_ref, w_tg_ref, w_to_ref, w_qkv_ref, w_ab_ref, w_ag_ref, w_ao_ref),
+            )
+        )
+    ]
+    for load in loads:
+        load.start()
     rows, res, cz = pair_ref.shape
+    side = math.isqrt(n // 2)
     me = lax.axis_index("rows")
     core = lax.rem(me, 2)
+    x = me // (2 * side)
+    y = lax.rem(me // 2, side)
     partner = me + 1 - 2 * core
+    lead = x + core * (y - x)
+    far = sorted(range(1, side), key=lambda t: -min(t, side - t))
+    near = sorted(range(1, side), key=lambda t: min(t, side - t))
+
+    def chip(tx, ty):
+        return lax.rem(x + tx, side) * side + lax.rem(y + ty, side)
 
     barrier = pltpu.get_barrier_semaphore()
 
-    def peer(t):
-        return lax.rem(me + t, n)
-
-    def greet(t, carry):
-        pl.semaphore_signal(barrier, inc=1, device_id={"rows": peer(t)}, device_id_type=MESH)
-        return carry
-
-    lax.fori_loop(1, n, greet, 0)
-
-    def exchange(source, target, k):
-        def send(t, carry):
-            d = peer(t)
-            pltpu.make_async_remote_copy(
-                src_ref=source(d), dst_ref=target, send_sem=send_sem.at[k], recv_sem=recv_sem.at[k],
-                device_id={"rows": d}, device_id_type=MESH,
-            ).start()
-            return carry
-
-        lax.fori_loop(1, n, send, 0)
-        pltpu.make_async_copy(source(me), target, recv_sem.at[k]).start()
-
-    def to_partner(source, target, k):
+    def greet(device):
+        pl.semaphore_signal(barrier, inc=1, device_id={"rows": device}, device_id_type=MESH)
+
+    for t in far:
+        for c in range(2):
+            greet(2 * chip(t, 0) + c)
+            greet(2 * chip(0, t) + c)
+    greet(partner)
+
+    def push(source, target, sent, received, device):
         copy = pltpu.make_async_remote_copy(
-            src_ref=source, dst_ref=target, send_sem=send_sem.at[k], recv_sem=recv_sem.at[k],
-            device_id={"rows": partner}, device_id_type=MESH,
+            src_ref=source, dst_ref=target, send_sem=send_sem.at[sent], recv_sem=received,
+            device_id={"rows": device}, device_id_type=MESH,
         )
         copy.start()
-        return copy
+
+    def first_leg(send_ref, mid_ref, sent, sems):
+        @pl.when(core == 0)
+        def _():
+            for t in far:
+                push(
+                    send_ref.at[lax.rem(x + t, side)], mid_ref.at[x], sent, sems.at[(side - t) % side],
+                    2 * chip(t, 0),
+                )
+
+        @pl.when(core == 1)
+        def _():
+            for t in far:
+                push(
+                    send_ref.at[:, lax.rem(y + t, side)], mid_ref.at[y], sent, sems.at[(side - t) % side],
+                    2 * chip(0, t) + 1,
+                )
+
+    def second_leg(send_ref, mid_ref, recv_ref, sent, sems, received):
+        for u in [0] + near:
+            s = lax.rem(lead + u, side)
+            if u:
+                whole_wait(mid_ref.at[s], sems.at[u])
+            origin = (s + core * (x - s)) * 2 * side + (y + core * (s - y)) * 2 + core
+            for t in far + [0]:
+                tx, ty = core * t, (1 - core) * t
+                across = lax.rem(y + core * (x - y) + t, side)
+                for dc in range(2):
+                    c = core + dc - 2 * core * dc
+                    if u:
+                        source = mid_ref.at[s, across, c]
+                    else:
+                        source = send_ref.at[lax.rem(x + tx, side), lax.rem(y + ty, side), c]
+                    if t or dc:
+                        push(source, recv_ref.at[origin], sent, received, 2 * chip(tx, ty) + c)
+                    else:
+                        pltpu.make_async_copy(source, recv_ref.at[origin], received).start()
+
+    def exchange(source, target, k):
+        for tx, ty, tc in far_first(side):
+            d = 2 * chip(tx, ty) + core + tc - 2 * core * tc
+            push(source(d), target, k, recv_sem.at[k], d)
+        pltpu.make_async_copy(source(me), target, recv_sem.at[k]).start()
+
+    def to_partner(source, target, k):
+        push(source, target, k, recv_sem.at[k], partner)
+
+    for load in loads:
+        load.wait()
 
     key_mask = mask_ref[...].astype(F32)
     lane = iota((1, res), 1)
@@ -96,7 +153,8 @@
         jnp.sum(jnp.where(lane == me * rows + r, key_mask, 0.0), axis=1, keepdims=True) for r in range(rows)
     ]
     spreads = [spread_rows(2 * cz, cz, r) for r in range(2)]
-    pair_send[...] = pair_ref[...].reshape(rows, n, 2, cz)
+    for r in range(rows):
+        pair_send[:, :, :, r] = pair_ref[r].reshape(side, side, 2, 2, cz)
     normed = jnp.concatenate(
         [norm_lanes(pair_ref[r].astype(F32)).astype(BF) for r in range(rows)], axis=1
     )
@@ -110,11 +168,13 @@
     pair_mask = jnp.where(parity == 0, row_mask[0], row_mask[1]) * key_mask
     for a in range(2):
         edge = (sigmoid(projected(2 * a)) * projected(2 * a + 1) * pair_mask).astype(BF)
-        edge_send[:, a] = edge.reshape(n, 2, res)
-
-    pl.semaphore_wait(barrier, n - 1)
-    exchange(lambda d: edge_send.at[d], edge_recv.at[me], 0)
-    exchange(lambda d: pair_send.at[:, d], pair_recv.at[me], 1)
+        edge_send[:, :, :, a] = edge.reshape(side, side, 2, 2, res)
+
+    pl.semaphore_wait(barrier, 4 * side - 3)
+    first_leg(edge_send, edge_mid, 8, edge_sem)
+    first_leg(pair_send, pair_mid, 9, pair_sem)
+    second_leg(edge_send, edge_mid, edge_recv, 0, edge_sem, recv_sem.at[0])
+    second_leg(pair_send, pair_mid, pair_recv, 1, pair_sem, recv_sem.at[1])
 
     whole_wait(edge_recv, recv_sem.at[0])
     left = edge_recv[:, 0].reshape(res, res)
@@ -160,24 +220,46 @@
     to_partner(att_own, att_peer, 4)
     both = jnp.concatenate([att_own[0], att_own[1]], axis=1)
     bias_send[...] = dot(w_bias, both, NT).reshape(2, 4, res)
-    exchange(lambda d: bias_send.at[lax.rem(d, 2)], bias_recv.at[me], 3)
+    for t in far:
+        push(bias_send.at[0], bias_recv.at[me], 3, bias_sem.at[(side - t) % side], 2 * chip(t, 0))
+        push(bias_send.at[1], bias_recv.at[me], 3, bias_sem.at[(side - t) % side], 2 * chip(0, t) + 1)
+    push(bias_send.at[1 - core], bias_recv.at[me], 3, bias_sem.at[0], partner)
+    pltpu.make_async_copy(bias_send.at[core], bias_recv.at[me], bias_sem.at[0]).start()
+
+    def pass_on(u):
+        s = lax.rem(lead + u, side)
+        block = bias_recv.at[pl.ds(2 * ((s + core * (x - s)) * side + y + core * (s - y)), 2)]
+        whole_wait(block, bias_sem.at[u])
+        for t in far:
+            push(block, block, 10, recv_sem.at[3], 2 * chip(core * t, (1 - core) * t) + core)
 
     penalty = (key_mask - 1.0) * MASK_PENALTY
     lane_head = iota((1, cz), 1) // HEAD_DIM
     head_mask = [lane_head == 2 * core + h for h in range(2)]
     values = []
-    for l in range(4):
-        if l == 2:
-            whole_wait(att_peer, recv_sem.at[4])
-        x = att_own[l] if l < 2 else att_peer[l - 2]
-        qkv = dot(x, w_qkv_ref[...]).astype(BF)
+
+    def score(rows_in):
+        qkv = dot(rows_in, w_qkv_ref[...]).astype(BF)
         for h in range(2):
             key = jnp.where(head_mask[h], qkv[:, cz : 2 * cz], 0)
-            scores[2 * l + h] = dot(qkv[:, :cz], key, NT) * (HEAD_DIM ** -0.5) + penalty
+            scores[2 * len(values) + h] = dot(qkv[:, :cz], key, NT) * (HEAD_DIM ** -0.5) + penalty
         values.append(qkv[:, 2 * cz :])
+
+    score(att_own[0])
+    pass_on(0)
+    score(att_own[1])
+    whole_wait(att_peer, recv_sem.at[4])
+    pass_on(near[0])
+    pass_on(near[1])
+    score(att_peer[0])
+    pass_on(near[2])
+    pass_on(near[3])
+    score(att_peer[1])
+    for u in near[4:]:
+        pass_on(u)
     att_gates = [sigmoid(dot(att_own[jj], w_ag_ref[...])) for jj in range(2)]
 
-    whole_wait(bias_recv, recv_sem.at[3])
+    whole_wait(bias_recv.at[pl.ds(0, n - 2 * side)], recv_sem.at[3])
     any_head = head_mask[0] | head_mask[1]
 
     def attended(l):
@@ -206,29 +288,38 @@
     out_ref[...] = upd_recv[...].reshape(rows, res, cz)
 
     others = pl.ds(0, n - 1)
-    whole_wait(edge_recv.at[others], send_sem.at[0])
-    whole_wait(pair_recv.at[others], send_sem.at[1])
+    passed = pl.ds(0, n - side)
+    whole_wait(edge_recv.at[passed], send_sem.at[0])
+    whole_wait(pair_recv.at[passed], send_sem.at[1])
     whole_wait(prod_recv.at[others], send_sem.at[2])
-    whole_wait(bias_recv.at[others], send_sem.at[3])
+    whole_wait(bias_recv.at[pl.ds(0, 2 * side - 1)], send_sem.at[3])
     whole_wait(att_peer, send_sem.at[4])
     whole_wait(o_recv.at[0], send_sem.at[5])
     whole_wait(o_recv.at[1], send_sem.at[6])
     whole_wait(upd_recv.at[:, others], send_sem.at[7])
-
-
-def local(n, pair, mask, w_tri_in, w_tri_gate, w_tri_out, w_qkv, w_att_bias, w_att_gate, w_att_out):
-    rows, res, cz = pair.shape
-    vmem = pl.BlockSpec(memory_space=pltpu.VMEM)
+    whole_wait(edge_mid.at[pl.ds(0, side - 1)], send_sem.at[8])
+    whole_wait(pair_mid.at[pl.ds(0, side - 1)], send_sem.at[9])
+    whole_wait(bias_recv.at[pl.ds(0, n - 2 * side)], send_sem.at[10])
+
+def local(n, *args):
+    args = [args[0], args[1].reshape(1, -1), *args[2:]]
+    rows, res, cz = args[0].shape
+    side = math.isqrt(n // 2)
+    pair_grid = (side, side, 2, rows, 2, cz)
+    edge_grid = (side, side, 2, 2, 2, res)
     return pl.pallas_call(
         functools.partial(kernel, n),
-        out_shape=jax.ShapeDtypeStruct(pair.shape, BF),
-        in_specs=[vmem] * 9,
-        out_specs=vmem,
-        scratch_shapes=[
-            pltpu.VMEM((rows, n, 2, cz), BF),
+        out_shape=jax.ShapeDtypeStruct(args[0].shape, BF),
+        in_specs=[pl.BlockSpec(memory_space=pl.ANY)] * len(args),
+        out_specs=pl.BlockSpec(memory_space=pltpu.VMEM),
+        scratch_shapes=[pltpu.VMEM(a.shape, a.dtype) for a in args]
+        + [
+            pltpu.VMEM(pair_grid, BF),
+            pltpu.VMEM(pair_grid, BF),
+            pltpu.VMEM((n, rows, 2, cz), BF),
+            pltpu.VMEM(edge_grid, BF),
+            pltpu.VMEM(edge_grid, BF),
             pltpu.VMEM((n, 2, 2, res), BF),
-            pltpu.VMEM((n, 2, 2, res), BF),
-            pltpu.VMEM((n, rows, 2, cz), BF),
             pltpu.VMEM((n, 2, res), BF),
             pltpu.VMEM((n, 2, res), BF),
             pltpu.VMEM((2 * res, cz), F32),
@@ -243,13 +334,16 @@
             pltpu.VMEM((2, res, cz), BF),
             pltpu.VMEM((n, rows, 2, cz), BF),
             pltpu.VMEM((rows, n, 2, cz), BF),
+            pltpu.SemaphoreType.DMA((len(args),)),
+            pltpu.SemaphoreType.DMA((11,)),
             pltpu.SemaphoreType.DMA((8,)),
-            pltpu.SemaphoreType.DMA((8,)),
+            pltpu.SemaphoreType.DMA((side,)),
+            pltpu.SemaphoreType.DMA((side,)),
+            pltpu.SemaphoreType.DMA((side,)),
         ],
         compiler_params=pltpu.CompilerParams(collective_id=0, has_side_effects=True),
         name="pair_update",
-    )(pair, mask.reshape(1, res), w_tri_in, w_tri_gate, w_tri_out, w_qkv, w_att_bias, w_att_gate, w_att_out)
-
+    )(*args)
 
 def solution(mesh):
     split = P(("parts", "rows"), None, None)

time: 81.8 us -> 71 us (0.87)
  Pallas kernels: 78.7 us -> 67.8 us
    pallas_call x1, Pallas kernels: 78.7 us -> 67.8 us  [local(): pl.pallas_call(functools.partial(kernel, n), out_shape=jax.ShapeDtypeStru...]
where the time goes in v3:
time: 71 us; the launch traced here: 70.8 us
  Pallas kernels  67.8 us (95%)
  local copies, waits for them, and re-layouts  2.98 us (4%)
    pallas_call x1, Pallas kernels, local(): pl.pallas_call(functools.partial(kernel, n), out_shape=jax.ShapeDtypeStru...  67.8 us
    unnamed x4, local copies, waits for them, and re-layouts  2.98 us

profile of v3, /device:TPU:513, one launch (start us, length us, event | category | flops | bytes accessed | tf_op | source)
XLA Modules:
  0.0 70.8 jit_solution(6623361965982105521)
XLA Ops:
  0.0 0.0 copy-start
  0.0 0.7 copy-done
  0.7 0.7 %copy.10.w_ab_hbm = bf16[128,4]{1,0:T(8,128)(2,1)} copy(bf16[128,4]{0,1:T(4,128)(2,1)S(1)} %copy-done) | data formatting | bytes 2048 | tf_op args[6]
  1.4 67.8 %pair_update.1 = bf16[2,256,128]{2,1,0:T(8,128)(2,1)} custom-call(bf16[2,256,128]{2,1,0:T(8,128)(2,1)} %pair_hbm.1, s32[1,256]{1,0:T(1,128)} %bitcast.1, bf16[128,512]{1,0:T(8,128)(2,1)} %w_in_hbm.1, bf16[128,128]{1,0:T(8,128)(2,1)} %w_tg_hbm.1, bf16[128,128]{1,0:T(8,128)(2,1)} %w_to_hbm.1, bf16[128,384]{1,0:T(8,128)(2,1)} %w_qkv_hbm.1, ...), custom_call_target="tpu_custom_call" | custom-call | tf_op jit(solution)/shard_map/pair_update/pallas_call | solution.py:310
  69.2 1.6 %copy.12 = bf16[2,256,128]{2,1,0:T(8,128)(2,1)} copy(bf16[2,256,128]{2,1,0:T(8,128)(2,1)} %pair_update.1) | data formatting | bytes 262144
Async XLA Ops:
  0.0 0.7 copy-start

commit v4 on v3

--- a/solution.py
+++ b/solution.py
@@ -53,7 +53,7 @@
     pair_ref, mask_ref, w_in_ref, w_tg_ref, w_to_ref, w_qkv_ref, w_ab_ref, w_ag_ref, w_ao_ref,
     pair_send, pair_mid, pair_recv, edge_send, edge_mid, edge_recv, prod_send, prod_recv,
     tokens, middle, att_own, att_peer, bias_send, bias_recv, scores, o_send, o_recv, o_own, upd_send, upd_recv,
-    load_sem, send_sem, recv_sem, edge_sem, pair_sem, bias_sem,
+    load_sem, send_sem, recv_sem, edge_sem, pair_sem, bias_sem, ready_sem, late_sem,
 ):
     loads = [
         pltpu.make_async_copy(hbm, ref, load_sem.at[i])
@@ -85,11 +85,30 @@
     def greet(device):
         pl.semaphore_signal(barrier, inc=1, device_id={"rows": device}, device_id_type=MESH)
 
-    for t in far:
-        for c in range(2):
-            greet(2 * chip(t, 0) + c)
-            greet(2 * chip(0, t) + c)
-    greet(partner)
+    first = me == 0
+    beside_first = me == 1
+    in_row = (y == 0) & (x > 0)
+    in_column = (x == 0) & (y > 0)
+    feeds_first = in_row & (core == 0)
+    ends_at_first = (in_column & (core == 0)) | (in_row & (core == 1))
+
+    @pl.when(me > 0)
+    def _():
+        for t in far:
+            greet(2 * chip(t, 0))
+            greet(2 * chip(0, t) + 1)
+        greet(partner)
+
+    def tell(sem, device):
+        pl.semaphore_signal(sem, inc=1, device_id={"rows": device}, device_id_type=MESH)
+
+    @pl.when(first)
+    def _():
+        pl.semaphore_wait(barrier, 2 * side - 1)
+        tell(ready_sem, 1)
+        for t in far:
+            for c in range(2):
+                tell(late_sem, 2 * side * t + c)
 
     def push(source, target, sent, received, device):
         copy = pltpu.make_async_remote_copy(
@@ -102,10 +121,14 @@
         @pl.when(core == 0)
         def _():
             for t in far:
-                push(
-                    send_ref.at[lax.rem(x + t, side)], mid_ref.at[x], sent, sems.at[(side - t) % side],
-                    2 * chip(t, 0),
-                )
+                target = lax.rem(x + t, side)
+
+                @pl.when((y > 0) | (target > 0))
+                def _():
+                    push(
+                        send_ref.at[target], mid_ref.at[x], sent, sems.at[(side - t) % side],
+                        2 * (target * side + y),
+                    )
 
         @pl.when(core == 1)
         def _():
@@ -115,25 +138,57 @@
                     2 * chip(0, t) + 1,
                 )
 
-    def second_leg(send_ref, mid_ref, recv_ref, sent, sems, received):
-        for u in [0] + near:
+    def first_leg_late(send_ref, mid_ref, sent, sems):
+        push(send_ref.at[0], mid_ref.at[x], sent, sems.at[x], 0)
+
+    late_u = jnp.where(feeds_first, side - x, side // 2)
+
+    def offset(k):
+        u = lax.rem(side + jnp.where(lax.rem(k, 2) == 1, (k + 1) // 2, -(k // 2)), side)
+        u = jnp.where(u == late_u, side // 2, u)
+        return jnp.where(k == side - 1, late_u, u)
+
+    def origin_of(s):
+        return (s + core * (x - s)) * 2 * side + (y + core * (s - y)) * 2 + core
+
+    def second_leg(k, u, send_ref, mid_ref, recv_ref, sent, sems, received):
+        s = lax.rem(lead + u, side)
+        if k is not None:
+            whole_wait(mid_ref.at[s], sems.at[u])
+        for t in far + [0]:
+            tx, ty = core * t, (1 - core) * t
+            across = lax.rem(y + core * (x - y) + t, side)
+            for dc in range(2):
+                c = core + dc - 2 * core * dc
+                if k is not None:
+                    source = mid_ref.at[s, across, c]
+                else:
+                    source = send_ref.at[lax.rem(x + tx, side), lax.rem(y + ty, side), c]
+                if t:
+                    device = 2 * chip(tx, ty) + c
+
+                    @pl.when(device > 0)
+                    def _():
+                        push(source, recv_ref.at[origin_of(s)], sent, received, device)
+                elif dc:
+                    push(source, recv_ref.at[origin_of(s)], sent, received, partner)
+                else:
+                    pltpu.make_async_copy(source, recv_ref.at[origin_of(s)], received).start()
+
+    def second_leg_late(send_ref, mid_ref, recv_ref, sent, received):
+        push(send_ref.at[0, 0, 0], recv_ref.at[me], sent, received, 0)
+        for u in range(1, side):
             s = lax.rem(lead + u, side)
-            if u:
-                whole_wait(mid_ref.at[s], sems.at[u])
-            origin = (s + core * (x - s)) * 2 * side + (y + core * (s - y)) * 2 + core
-            for t in far + [0]:
-                tx, ty = core * t, (1 - core) * t
-                across = lax.rem(y + core * (x - y) + t, side)
-                for dc in range(2):
-                    c = core + dc - 2 * core * dc
-                    if u:
-                        source = mid_ref.at[s, across, c]
-                    else:
-                        source = send_ref.at[lax.rem(x + tx, side), lax.rem(y + ty, side), c]
-                    if t or dc:
-                        push(source, recv_ref.at[origin], sent, received, 2 * chip(tx, ty) + c)
-                    else:
-                        pltpu.make_async_copy(source, recv_ref.at[origin], received).start()
+            push(mid_ref.at[s, 0, 0], recv_ref.at[origin_of(s)], sent, received, 0)
+
+    def second_legs(*refs):
+        second_leg(None, 0, *refs)
+
+        def step(k, carry):
+            second_leg(k, offset(k), *refs)
+            return carry
+
+        lax.fori_loop(1, side - 1, step, 0)
 
     def exchange(source, target, k):
         for tx, ty, tc in far_first(side):
@@ -170,17 +225,57 @@
         edge = (sigmoid(projected(2 * a)) * projected(2 * a + 1) * pair_mask).astype(BF)
         edge_send[:, :, :, a] = edge.reshape(side, side, 2, 2, res)
 
-    pl.semaphore_wait(barrier, 4 * side - 3)
+    @pl.when(me > 0)
+    def _():
+        absent = feeds_first | ((x == 0) & (core == 1))
+        pl.semaphore_wait(barrier, 2 * side - 1 - absent.astype(jnp.int32))
+
+        @pl.when(me > 1)
+        def _():
+            tell(ready_sem, partner)
+
+    edge_legs = (edge_send, edge_mid, edge_recv, 0, edge_sem, recv_sem.at[0])
+    pair_legs = (pair_send, pair_mid, pair_recv, 1, pair_sem, recv_sem.at[1])
     first_leg(edge_send, edge_mid, 8, edge_sem)
+    pl.semaphore_wait(ready_sem, 1)
+
+    @pl.when(beside_first)
+    def _():
+        tell(ready_sem, 0)
+
+    @pl.when(first)
+    def _():
+        for t in far:
+            tell(late_sem, 2 * t)
+
+    second_legs(*edge_legs)
     first_leg(pair_send, pair_mid, 9, pair_sem)
-    second_leg(edge_send, edge_mid, edge_recv, 0, edge_sem, recv_sem.at[0])
-    second_leg(pair_send, pair_mid, pair_recv, 1, pair_sem, recv_sem.at[1])
+
+    @pl.when(feeds_first)
+    def _():
+        pl.semaphore_wait(late_sem, 1)
+        first_leg_late(edge_send, edge_mid, 8, edge_sem)
+        first_leg_late(pair_send, pair_mid, 9, pair_sem)
+
+    second_leg(side - 1, late_u, *edge_legs)
+
+    @pl.when(ends_at_first)
+    def _():
+        pl.semaphore_wait(late_sem, 1)
+        second_leg_late(edge_send, edge_mid, edge_recv, 0, recv_sem.at[0])
 
     whole_wait(edge_recv, recv_sem.at[0])
     left = edge_recv[:, 0].reshape(res, res)
     right = edge_recv[:, 1].reshape(res, res)
     prod_send[...] = dot(right, left, NT).astype(BF).reshape(n, 2, res)
     exchange(lambda d: prod_send.at[d], prod_recv.at[me], 2)
+
+    second_legs(*pair_legs)
+    second_leg(side - 1, late_u, *pair_legs)
+
+    @pl.when(ends_at_first)
+    def _():
+        second_leg_late(pair_send, pair_mid, pair_recv, 1, recv_sem.at[1])
 
     whole_wait(pair_recv, recv_sem.at[1])
     tokens[...] = pair_recv[...].reshape(2 * res, cz).astype(F32)
@@ -192,7 +287,7 @@
     e_col = iota((8, HEADS), 1)
     w_bias = jnp.concatenate(
         [
-            dot(((e_row // 2 == e_col) & (e_row % 2 == jj)).astype(F32).astype(BF), w_ab_ref[...], NT).astype(BF)
+            dot(((e_row // 2 == e_col) & (e_row % 2 == jj)).astype(F32).astype(BF), w_ab_ref[...]).astype(BF)
             for jj in range(2)
         ],
         axis=1,
@@ -302,14 +397,14 @@
     whole_wait(bias_recv.at[pl.ds(0, n - 2 * side)], send_sem.at[10])
 
 def local(n, *args):
-    args = [args[0], args[1].reshape(1, -1), *args[2:]]
+    args = [args[0], args[1].reshape(1, -1), *args[2:6], args[6].T, *args[7:]]
     rows, res, cz = args[0].shape
     side = math.isqrt(n // 2)
     pair_grid = (side, side, 2, rows, 2, cz)
     edge_grid = (side, side, 2, 2, 2, res)
     return pl.pallas_call(
         functools.partial(kernel, n),
-        out_shape=jax.ShapeDtypeStruct(args[0].shape, BF),
+        out_shape=pltpu.VMEM(args[0].shape, BF),
         in_specs=[pl.BlockSpec(memory_space=pl.ANY)] * len(args),
         out_specs=pl.BlockSpec(memory_space=pltpu.VMEM),
         scratch_shapes=[pltpu.VMEM(a.shape, a.dtype) for a in args]
@@ -340,6 +435,8 @@
             pltpu.SemaphoreType.DMA((side,)),
             pltpu.SemaphoreType.DMA((side,)),
             pltpu.SemaphoreType.DMA((side,)),
+            pltpu.SemaphoreType.REGULAR,
+            pltpu.SemaphoreType.REGULAR,
         ],
         compiler_params=pltpu.CompilerParams(collective_id=0, has_side_effects=True),
         name="pair_update",

time: 71 us -> 67.2 us (0.946)
  local copies, waits for them, and re-layouts: 2.98 us -> 0.66 us
  Pallas kernels: 67.8 us -> 66.4 us
    unnamed x4 -> x1, local copies, waits for them, and re-layouts: 2.98 us -> 0.66 us
    pallas_call x1, Pallas kernels: 67.8 us -> 66.4 us  [local(): pl.pallas_call(functools.partial(kernel, n), out_shape=pltpu.VMEM(args[0]...]
where the time goes in v4:
time: 67.2 us; the launch traced here: 67.1 us
  Pallas kernels  66.4 us (99%)
    pallas_call x1, Pallas kernels, local(): pl.pallas_call(functools.partial(kernel, n), out_shape=pltpu.VMEM(args[0]...  66.4 us

profile of v4, /device:TPU:513, one launch (start us, length us, event | category | flops | bytes accessed | tf_op | source)
XLA Modules:
  0.0 67.1 jit_solution(11638089722587409198)
XLA Ops:
  0.0 66.4 %pair_update.1 = bf16[2,256,128]{2,1,0:T(8,128)(2,1)S(1)} custom-call(bf16[2,256,128]{2,1,0:T(8,128)(2,1)} %pair_hbm.1, s32[1,256]{1,0:T(1,128)} %bitcast.2, bf16[128,512]{1,0:T(8,128)(2,1)} %w_in_hbm.1, bf16[128,128]{1,0:T(8,128)(2,1)} %w_tg_hbm.1, bf16[128,128]{1,0:T(8,128)(2,1)} %w_to_hbm.1, bf16[128,384]{1,0:T(8,128)(2,1)} %w_qkv_hbm.1, ...), custom_call_target="tpu_custom_call" | custom-call | tf_op jit(solution)/shard_map/pair_update/pallas_call | solution.py:405
  66.4 0.7 copy.11

commit v5 on v4

--- a/solution.py
+++ b/solution.py
@@ -181,6 +181,31 @@
             s = lax.rem(lead + u, side)
             push(mid_ref.at[s, 0, 0], recv_ref.at[origin_of(s)], sent, received, 0)
 
+    def second_leg_at_once(send_ref, mid_ref, recv_ref, sent, sems, received):
+        @pl.when(core == 0)
+        def _():
+            pltpu.make_async_copy(send_ref.at[x], mid_ref.at[x], sems.at[0]).start()
+
+        @pl.when(core == 1)
+        def _():
+            pltpu.make_async_copy(send_ref.at[:, y], mid_ref.at[y], sems.at[0]).start()
+
+        for u in range(side):
+            whole_wait(mid_ref.at[lax.rem(lead + u, side)], sems.at[u])
+        for along in range(2):
+
+            @pl.when(core == along)
+            def _():
+                target = recv_ref.at[x, :, 1] if along else recv_ref.at[:, y, 0]
+                for t in far + [0]:
+                    across = lax.rem((x if along else y) + t, side)
+                    for c in range(2):
+                        source = mid_ref.at[:, across, c]
+                        if t or c != along:
+                            push(source, target, sent, received, 2 * (chip(t, 0) if along else chip(0, t)) + c)
+                        else:
+                            pltpu.make_async_copy(source, target, received).start()
+
     def second_legs(*refs):
         second_leg(None, 0, *refs)
 
@@ -264,18 +289,13 @@
         pl.semaphore_wait(late_sem, 1)
         second_leg_late(edge_send, edge_mid, edge_recv, 0, recv_sem.at[0])
 
+    second_leg_at_once(*pair_legs)
+
     whole_wait(edge_recv, recv_sem.at[0])
     left = edge_recv[:, 0].reshape(res, res)
     right = edge_recv[:, 1].reshape(res, res)
     prod_send[...] = dot(right, left, NT).astype(BF).reshape(n, 2, res)
     exchange(lambda d: prod_send.at[d], prod_recv.at[me], 2)
-
-    second_legs(*pair_legs)
-    second_leg(side - 1, late_u, *pair_legs)
-
-    @pl.when(ends_at_first)
-    def _():
-        second_leg_late(pair_send, pair_mid, pair_recv, 1, recv_sem.at[1])
 
     whole_wait(pair_recv, recv_sem.at[1])
     tokens[...] = pair_recv[...].reshape(2 * res, cz).astype(F32)
@@ -385,7 +405,7 @@
     others = pl.ds(0, n - 1)
     passed = pl.ds(0, n - side)
     whole_wait(edge_recv.at[passed], send_sem.at[0])
-    whole_wait(pair_recv.at[passed], send_sem.at[1])
+    whole_wait(upd_send.at[passed], send_sem.at[1])
     whole_wait(prod_recv.at[others], send_sem.at[2])
     whole_wait(bias_recv.at[pl.ds(0, 2 * side - 1)], send_sem.at[3])
     whole_wait(att_peer, send_sem.at[4])
@@ -411,7 +431,7 @@
         + [
             pltpu.VMEM(pair_grid, BF),
             pltpu.VMEM(pair_grid, BF),
-            pltpu.VMEM((n, rows, 2, cz), BF),
+            pltpu.VMEM(pair_grid, BF),
             pltpu.VMEM(edge_grid, BF),
             pltpu.VMEM(edge_grid, BF),
             pltpu.VMEM((n, 2, 2, res), BF),

time: 67.2 us -> 63.4 us (0.943)
  Pallas kernels: 66.4 us -> 62.6 us
    pallas_call x1, Pallas kernels: 66.4 us -> 62.6 us  [local(): pl.pallas_call(functools.partial(kernel, n), out_shape=pltpu.VMEM(args[0]...]
where the time goes in v5:
time: 63.4 us; the launch traced here: 63.3 us
  Pallas kernels  62.6 us (99%)
  local copies, waits for them, and re-layouts  0.66 us (1%)
    pallas_call x1, Pallas kernels, local(): pl.pallas_call(functools.partial(kernel, n), out_shape=pltpu.VMEM(args[0]...  62.6 us

profile of v5, /device:TPU:513, one launch (start us, length us, event | category | flops | bytes accessed | tf_op | source)
XLA Modules:
  0.0 63.3 jit_solution(13242054179158752684)
XLA Ops:
  0.0 62.6 %pair_update.1 = bf16[2,256,128]{2,1,0:T(8,128)(2,1)S(1)} custom-call(bf16[2,256,128]{2,1,0:T(8,128)(2,1)} %pair_hbm.1, s32[1,256]{1,0:T(1,128)} %bitcast.2, bf16[128,512]{1,0:T(8,128)(2,1)} %w_in_hbm.1, bf16[128,128]{1,0:T(8,128)(2,1)} %w_tg_hbm.1, bf16[128,128]{1,0:T(8,128)(2,1)} %w_to_hbm.1, bf16[128,384]{1,0:T(8,128)(2,1)} %w_qkv_hbm.1, ...), custom_call_target="tpu_custom_call" | custom-call | tf_op jit(solution)/shard_map/pair_update/pallas_call | solution.py:425
  62.6 0.7 %copy.11 = bf16[2,256,128]{2,1,0:T(8,128)(2,1)} copy(bf16[2,256,128]{2,1,0:T(8,128)(2,1)S(1)} %pair_update.1) | data formatting | bytes 262144

commit v6 on v5

--- a/solution.py
+++ b/solution.py
@@ -106,9 +106,11 @@
     def _():
         pl.semaphore_wait(barrier, 2 * side - 1)
         tell(ready_sem, 1)
+        pl.semaphore_wait(ready_sem, 1)
         for t in far:
             for c in range(2):
                 tell(late_sem, 2 * side * t + c)
+            tell(late_sem, 2 * t)
 
     def push(source, target, sent, received, device):
         copy = pltpu.make_async_remote_copy(
@@ -138,50 +140,12 @@
                     2 * chip(0, t) + 1,
                 )
 
-    def first_leg_late(send_ref, mid_ref, sent, sems):
-        push(send_ref.at[0], mid_ref.at[x], sent, sems.at[x], 0)
-
-    late_u = jnp.where(feeds_first, side - x, side // 2)
-
-    def offset(k):
-        u = lax.rem(side + jnp.where(lax.rem(k, 2) == 1, (k + 1) // 2, -(k // 2)), side)
-        u = jnp.where(u == late_u, side // 2, u)
-        return jnp.where(k == side - 1, late_u, u)
-
-    def origin_of(s):
-        return (s + core * (x - s)) * 2 * side + (y + core * (s - y)) * 2 + core
-
-    def second_leg(k, u, send_ref, mid_ref, recv_ref, sent, sems, received):
-        s = lax.rem(lead + u, side)
-        if k is not None:
-            whole_wait(mid_ref.at[s], sems.at[u])
+    def around_first(send_ref, recv_ref, sent, received):
         for t in far + [0]:
-            tx, ty = core * t, (1 - core) * t
-            across = lax.rem(y + core * (x - y) + t, side)
-            for dc in range(2):
-                c = core + dc - 2 * core * dc
-                if k is not None:
-                    source = mid_ref.at[s, across, c]
-                else:
-                    source = send_ref.at[lax.rem(x + tx, side), lax.rem(y + ty, side), c]
-                if t:
-                    device = 2 * chip(tx, ty) + c
-
-                    @pl.when(device > 0)
-                    def _():
-                        push(source, recv_ref.at[origin_of(s)], sent, received, device)
-                elif dc:
-                    push(source, recv_ref.at[origin_of(s)], sent, received, partner)
-                else:
-                    pltpu.make_async_copy(source, recv_ref.at[origin_of(s)], received).start()
-
-    def second_leg_late(send_ref, mid_ref, recv_ref, sent, received):
-        push(send_ref.at[0, 0, 0], recv_ref.at[me], sent, received, 0)
-        for u in range(1, side):
-            s = lax.rem(lead + u, side)
-            push(mid_ref.at[s, 0, 0], recv_ref.at[origin_of(s)], sent, received, 0)
-
-    def second_leg_at_once(send_ref, mid_ref, recv_ref, sent, sems, received):
+            for c in range(2):
+                push(send_ref.at[0, t, c], recv_ref.at[x, 0, 0], sent, received, 2 * t + c)
+
+    def own_leg(send_ref, mid_ref, sems):
         @pl.when(core == 0)
         def _():
             pltpu.make_async_copy(send_ref.at[x], mid_ref.at[x], sems.at[0]).start()
@@ -190,30 +154,38 @@
         def _():
             pltpu.make_async_copy(send_ref.at[:, y], mid_ref.at[y], sems.at[0]).start()
 
-        for u in range(side):
-            whole_wait(mid_ref.at[lax.rem(lead + u, side)], sems.at[u])
+    def second_leg(low, high, mid_ref, recv_ref, sent, sems, received, skip_first):
+        span = pl.ds(low, high - low)
+        for s in range(low, high):
+            whole_wait(mid_ref.at[s], sems.at[lax.rem(s - lead + side, side)])
         for along in range(2):
 
             @pl.when(core == along)
             def _():
-                target = recv_ref.at[x, :, 1] if along else recv_ref.at[:, y, 0]
+                target = recv_ref.at[x, span, 1] if along else recv_ref.at[span, y, 0]
                 for t in far + [0]:
                     across = lax.rem((x if along else y) + t, side)
-                    for c in range(2):
-                        source = mid_ref.at[:, across, c]
-                        if t or c != along:
-                            push(source, target, sent, received, 2 * (chip(t, 0) if along else chip(0, t)) + c)
+                    there = 2 * (chip(t, 0) if along else chip(0, t))
+                    for c in (1 - along, along):
+                        source = mid_ref.at[span, across, c]
+                        if t and c == 0 and skip_first:
+
+                            @pl.when(there > 0)
+                            def _():
+                                push(source, target, sent, received, there)
+                        elif t or c != along:
+                            push(source, target, sent, received, there + c)
                         else:
                             pltpu.make_async_copy(source, target, received).start()
 
-    def second_legs(*refs):
-        second_leg(None, 0, *refs)
-
-        def step(k, carry):
-            second_leg(k, offset(k), *refs)
-            return carry
-
-        lax.fori_loop(1, side - 1, step, 0)
+    def second_leg_late(low, high, mid_ref, recv_ref, sent, received):
+        span = pl.ds(low, high - low)
+        for along in range(2):
+
+            @pl.when(core == along)
+            def _():
+                target = recv_ref.at[x, span, 1] if along else recv_ref.at[span, y, 0]
+                push(mid_ref.at[span, 0, 0], target, sent, received, 0)
 
     def exchange(source, target, k):
         for tx, ty, tc in far_first(side):
@@ -259,41 +231,52 @@
         def _():
             tell(ready_sem, partner)
 
-    edge_legs = (edge_send, edge_mid, edge_recv, 0, edge_sem, recv_sem.at[0])
-    pair_legs = (pair_send, pair_mid, pair_recv, 1, pair_sem, recv_sem.at[1])
+    edge_legs = (edge_mid, edge_recv, 0, edge_sem, recv_sem.at[0])
+    pair_legs = (pair_mid, pair_recv, 1, pair_sem, recv_sem.at[1])
+    spans = ((side // 2, side), (1, side // 2), (0, 1))
     first_leg(edge_send, edge_mid, 8, edge_sem)
-    pl.semaphore_wait(ready_sem, 1)
-
-    @pl.when(beside_first)
-    def _():
-        tell(ready_sem, 0)
+    own_leg(edge_send, edge_mid, edge_sem)
+    first_leg(pair_send, pair_mid, 9, pair_sem)
+    own_leg(pair_send, pair_mid, pair_sem)
+    @pl.when(me > 0)
+    def _():
+        pl.semaphore_wait(ready_sem, 1)
+
+        @pl.when(beside_first)
+        def _():
+            tell(ready_sem, 0)
+
+        for low, high in spans[:2]:
+            second_leg(low, high, *edge_legs, True)
+
+        @pl.when(feeds_first)
+        def _():
+            pl.semaphore_wait(late_sem, 1)
+            around_first(edge_send, edge_recv, 8, recv_sem.at[0])
+
+    second_leg(*spans[2], *edge_legs, True)
+
+    @pl.when(feeds_first)
+    def _():
+        around_first(pair_send, pair_recv, 9, recv_sem.at[1])
+
+    @pl.when(ends_at_first)
+    def _():
+        pl.semaphore_wait(late_sem, 1)
+        for low, high in spans:
+            second_leg_late(low, high, edge_mid, edge_recv, 0, recv_sem.at[0])
+
+    @pl.when(me > 0)
+    def _():
+        second_leg(0, side, *pair_legs, False)
 
     @pl.when(first)
     def _():
-        for t in far:
-            tell(late_sem, 2 * t)
-
-    second_legs(*edge_legs)
-    first_leg(pair_send, pair_mid, 9, pair_sem)
-
-    @pl.when(feeds_first)
-    def _():
-        pl.semaphore_wait(late_sem, 1)
-        first_leg_late(edge_send, edge_mid, 8, edge_sem)
-        first_leg_late(pair_send, pair_mid, 9, pair_sem)
-
-    second_leg(side - 1, late_u, *edge_legs)
-
-    @pl.when(ends_at_first)
-    def _():
-        pl.semaphore_wait(late_sem, 1)
-        second_leg_late(edge_send, edge_mid, edge_recv, 0, recv_sem.at[0])
-
-    second_leg_at_once(*pair_legs)
+        second_leg(0, 1, *pair_legs, False)
 
     whole_wait(edge_recv, recv_sem.at[0])
-    left = edge_recv[:, 0].reshape(res, res)
-    right = edge_recv[:, 1].reshape(res, res)
+    left = edge_recv[:, :, :, 0].reshape(res, res)
+    right = edge_recv[:, :, :, 1].reshape(res, res)
     prod_send[...] = dot(right, left, NT).astype(BF).reshape(n, 2, res)
     exchange(lambda d: prod_send.at[d], prod_recv.at[me], 2)
 
@@ -404,8 +387,17 @@
 
     others = pl.ds(0, n - 1)
     passed = pl.ds(0, n - side)
-    whole_wait(edge_recv.at[passed], send_sem.at[0])
-    whole_wait(upd_send.at[passed], send_sem.at[1])
+
+    @pl.when(me > 0)
+    def _():
+        whole_wait(bias_recv.at[pl.ds(0, (n - side) // 2)], send_sem.at[0])
+        whole_wait(upd_send.at[passed], send_sem.at[1])
+
+    @pl.when(first)
+    def _():
+        whole_wait(upd_send.at[pl.ds(0, 4 * side - 2)], send_sem.at[0])
+        whole_wait(upd_send.at[pl.ds(0, 2 * side - 1)], send_sem.at[1])
+
     whole_wait(prod_recv.at[others], send_sem.at[2])
     whole_wait(bias_recv.at[pl.ds(0, 2 * side - 1)], send_sem.at[3])
     whole_wait(att_peer, send_sem.at[4])
@@ -434,7 +426,7 @@
             pltpu.VMEM(pair_grid, BF),
             pltpu.VMEM(edge_grid, BF),
             pltpu.VMEM(edge_grid, BF),
-            pltpu.VMEM((n, 2, 2, res), BF),
+            pltpu.VMEM(edge_grid, BF),
             pltpu.VMEM((n, 2, res), BF),
             pltpu.VMEM((n, 2, res), BF),
             pltpu.VMEM((2 * res, cz), F32),

time: 63.4 us -> 62 us (0.978)
  Pallas kernels: 62.6 us -> 61.2 us
    pallas_call x1, Pallas kernels: 62.6 us -> 61.2 us  [local(): pl.pallas_call(functools.partial(kernel, n), out_shape=pltpu.VMEM(args[0]...]
where the time goes in v6:
time: 62 us; the launch traced here: 61.9 us
  Pallas kernels  61.2 us (99%)
  local copies, waits for them, and re-layouts  0.66 us (1%)
    pallas_call x1, Pallas kernels, local(): pl.pallas_call(functools.partial(kernel, n), out_shape=pltpu.VMEM(args[0]...  61.2 us

profile of v6, /device:TPU:513, one launch (start us, length us, event | category | flops | bytes accessed | tf_op | source)
XLA Modules:
  0.0 61.9 jit_solution(3296351223651755386)
XLA Ops:
  0.0 61.2 %pair_update.1 = bf16[2,256,128]{2,1,0:T(8,128)(2,1)S(1)} custom-call(bf16[2,256,128]{2,1,0:T(8,128)(2,1)} %pair_hbm.1, s32[1,256]{1,0:T(1,128)} %bitcast.2, bf16[128,512]{1,0:T(8,128)(2,1)} %w_in_hbm.1, bf16[128,128]{1,0:T(8,128)(2,1)} %w_tg_hbm.1, bf16[128,128]{1,0:T(8,128)(2,1)} %w_to_hbm.1, bf16[128,384]{1,0:T(8,128)(2,1)} %w_qkv_hbm.1, ...), custom_call_target="tpu_custom_call" | custom-call | tf_op jit(solution)/shard_map/pair_update/pallas_call | solution.py:417
  61.3 0.7 %copy.11 = bf16[2,256,128]{2,1,0:T(8,128)(2,1)} copy(bf16[2,256,128]{2,1,0:T(8,128)(2,1)S(1)} %pair_update.1) | data formatting | bytes 262144

commit v7 on v6

--- a/solution.py
+++ b/solution.py
@@ -53,7 +53,7 @@
     pair_ref, mask_ref, w_in_ref, w_tg_ref, w_to_ref, w_qkv_ref, w_ab_ref, w_ag_ref, w_ao_ref,
     pair_send, pair_mid, pair_recv, edge_send, edge_mid, edge_recv, prod_send, prod_recv,
     tokens, middle, att_own, att_peer, bias_send, bias_recv, scores, o_send, o_recv, o_own, upd_send, upd_recv,
-    load_sem, send_sem, recv_sem, edge_sem, pair_sem, bias_sem, ready_sem, late_sem,
+    load_sem, send_sem, recv_sem, edge_sem, pair_sem, bias_sem, ready_sem, late_sem, row_sem,
 ):
     loads = [
         pltpu.make_async_copy(hbm, ref, load_sem.at[i])
@@ -86,7 +86,6 @@
         pl.semaphore_signal(barrier, inc=1, device_id={"rows": device}, device_id_type=MESH)
 
     first = me == 0
-    beside_first = me == 1
     in_row = (y == 0) & (x > 0)
     in_column = (x == 0) & (y > 0)
     feeds_first = in_row & (core == 0)
@@ -95,22 +94,16 @@
     @pl.when(me > 0)
     def _():
         for t in far:
-            greet(2 * chip(t, 0))
+
+            @pl.when((y > 0) | (core == 1) | (lax.rem(x + t, side) > 0))
+            def _():
+                greet(2 * chip(t, 0))
+
             greet(2 * chip(0, t) + 1)
         greet(partner)
 
     def tell(sem, device):
         pl.semaphore_signal(sem, inc=1, device_id={"rows": device}, device_id_type=MESH)
-
-    @pl.when(first)
-    def _():
-        pl.semaphore_wait(barrier, 2 * side - 1)
-        tell(ready_sem, 1)
-        pl.semaphore_wait(ready_sem, 1)
-        for t in far:
-            for c in range(2):
-                tell(late_sem, 2 * side * t + c)
-            tell(late_sem, 2 * t)
 
     def push(source, target, sent, received, device):
         copy = pltpu.make_async_remote_copy(
@@ -143,7 +136,13 @@
     def around_first(send_ref, recv_ref, sent, received):
         for t in far + [0]:
             for c in range(2):
-                push(send_ref.at[0, t, c], recv_ref.at[x, 0, 0], sent, received, 2 * t + c)
+                if t or c:
+                    push(send_ref.at[0, t, c], recv_ref.at[x, 0, 0], sent, received, 2 * t + c)
+
+    def from_first(send_ref, recv_ref, sents, received):
+        for tx, ty, tc in far_first(side):
+            push(send_ref.at[tx, ty, tc], recv_ref.at[0, 0, 0], sents[tc], received, 2 * (tx * side + ty) + tc)
+        pltpu.make_async_copy(send_ref.at[0, 0, 0], recv_ref.at[0, 0, 0], received).start()
 
     def own_leg(send_ref, mid_ref, sems):
         @pl.when(core == 0)
@@ -196,7 +195,7 @@
     def to_partner(source, target, k):
         push(source, target, k, recv_sem.at[k], partner)
 
-    for load in loads:
+    for load in loads[:3]:
         load.wait()
 
     key_mask = mask_ref[...].astype(F32)
@@ -205,8 +204,6 @@
         jnp.sum(jnp.where(lane == me * rows + r, key_mask, 0.0), axis=1, keepdims=True) for r in range(rows)
     ]
     spreads = [spread_rows(2 * cz, cz, r) for r in range(2)]
-    for r in range(rows):
-        pair_send[:, :, :, r] = pair_ref[r].reshape(side, side, 2, 2, cz)
     normed = jnp.concatenate(
         [norm_lanes(pair_ref[r].astype(F32)).astype(BF) for r in range(rows)], axis=1
     )
@@ -234,45 +231,69 @@
     edge_legs = (edge_mid, edge_recv, 0, edge_sem, recv_sem.at[0])
     pair_legs = (pair_mid, pair_recv, 1, pair_sem, recv_sem.at[1])
     spans = ((side // 2, side), (1, side // 2), (0, 1))
-    first_leg(edge_send, edge_mid, 8, edge_sem)
-    own_leg(edge_send, edge_mid, edge_sem)
-    first_leg(pair_send, pair_mid, 9, pair_sem)
-    own_leg(pair_send, pair_mid, pair_sem)
+
+    @pl.when(first)
+    def _():
+        pl.semaphore_wait(barrier, 2 * side - 1)
+        tell(ready_sem, 1)
+        for t in far:
+            for c in range(2):
+                tell(late_sem, 2 * side * t + c)
+            tell(late_sem, 2 * t)
+        from_first(edge_send, edge_recv, (0, 8), recv_sem.at[0])
+
     @pl.when(me > 0)
     def _():
+        first_leg(edge_send, edge_mid, 8, edge_sem)
+        own_leg(edge_send, edge_mid, edge_sem)
+
+    for r in range(rows):
+        pair_send[:, :, :, r] = pair_ref[r].reshape(side, side, 2, 2, cz)
+    for load in loads[3:]:
+        load.wait()
+
+    @pl.when(first)
+    def _():
+        from_first(pair_send, pair_recv, (1, 1), recv_sem.at[1])
+
+    @pl.when(me > 0)
+    def _():
+        first_leg(pair_send, pair_mid, 9, pair_sem)
+        own_leg(pair_send, pair_mid, pair_sem)
         pl.semaphore_wait(ready_sem, 1)
 
-        @pl.when(beside_first)
-        def _():
-            tell(ready_sem, 0)
+        @pl.when((core == 0) & (x > 0) & (y > 0))
+        def _():
+            tell(row_sem, 2 * side * x)
+
+        @pl.when(feeds_first)
+        def _():
+            pl.semaphore_wait(row_sem, side - 1)
+            greet(0)
 
         for low, high in spans[:2]:
             second_leg(low, high, *edge_legs, True)
 
         @pl.when(feeds_first)
         def _():
+            around_first(edge_send, edge_recv, 8, recv_sem.at[0])
+            around_first(pair_send, pair_recv, 9, recv_sem.at[1])
             pl.semaphore_wait(late_sem, 1)
-            around_first(edge_send, edge_recv, 8, recv_sem.at[0])
-
-    second_leg(*spans[2], *edge_legs, True)
-
-    @pl.when(feeds_first)
-    def _():
-        around_first(pair_send, pair_recv, 9, recv_sem.at[1])
-
-    @pl.when(ends_at_first)
-    def _():
-        pl.semaphore_wait(late_sem, 1)
-        for low, high in spans:
-            second_leg_late(low, high, edge_mid, edge_recv, 0, recv_sem.at[0])
-
-    @pl.when(me > 0)
-    def _():
-        second_leg(0, side, *pair_legs, False)
-
-    @pl.when(first)
-    def _():
-        second_leg(0, 1, *pair_legs, False)
+            push(edge_send.at[0, 0, 0], edge_recv.at[x, 0, 0], 8, recv_sem.at[0], 0)
+            push(pair_send.at[0, 0, 0], pair_recv.at[x, 0, 0], 9, recv_sem.at[1], 0)
+            second_leg(1, side, *pair_legs, False)
+
+        @pl.when(jnp.logical_not(feeds_first))
+        def _():
+            second_leg(*spans[2], *edge_legs, True)
+
+            @pl.when(ends_at_first)
+            def _():
+                pl.semaphore_wait(late_sem, 1)
+                for low, high in spans:
+                    second_leg_late(low, high, edge_mid, edge_recv, 0, recv_sem.at[0])
+
+            second_leg(0, side, *pair_legs, False)
 
     whole_wait(edge_recv, recv_sem.at[0])
     left = edge_recv[:, :, :, 0].reshape(res, res)
@@ -376,9 +397,10 @@
     for jj in range(2):
         o_own[jj] = attended(jj)
     for jj in range(2):
+        middle[jj] = middle[jj] + dot((att_gates[jj] * o_own[jj].astype(F32)).astype(BF), w_ao_ref[...])
+    for jj in range(2):
         whole_wait(o_recv.at[jj], recv_sem.at[5 + jj])
-        att = o_own[jj].astype(F32) + o_recv[jj].astype(F32)
-        gated = (att_gates[jj] * att).astype(BF)
+        gated = (att_gates[jj] * o_recv[jj].astype(F32)).astype(BF)
         tokens[pl.ds(jj, res, stride=2), :] = middle[jj] + dot(gated, w_ao_ref[...])
     upd_send[...] = tokens[...].astype(BF).reshape(n, rows, 2, cz)
     exchange(lambda d: upd_send.at[d], upd_recv.at[:, me], 7)
@@ -388,15 +410,29 @@
     others = pl.ds(0, n - 1)
     passed = pl.ds(0, n - side)
 
+    half = pl.ds(0, res // 2)
+    ahead = (side - 1) * (2 * side - 1)
+
+    @pl.when(feeds_first)
+    def _():
+        whole_wait(bias_recv.at[pl.ds(0, ahead), :, half], send_sem.at[0])
+        whole_wait(upd_send.at[pl.ds(0, ahead)], send_sem.at[1])
+
+    @pl.when((me > 0) & jnp.logical_not(feeds_first))
+    def _():
+        whole_wait(bias_recv.at[passed, :, half], send_sem.at[0])
+        whole_wait(upd_send.at[passed], send_sem.at[1])
+
     @pl.when(me > 0)
     def _():
-        whole_wait(bias_recv.at[pl.ds(0, (n - side) // 2)], send_sem.at[0])
-        whole_wait(upd_send.at[passed], send_sem.at[1])
+        whole_wait(edge_mid.at[pl.ds(0, side - 1)], send_sem.at[8])
+        whole_wait(pair_mid.at[pl.ds(0, side - 1)], send_sem.at[9])
 
     @pl.when(first)
     def _():
-        whole_wait(upd_send.at[pl.ds(0, 4 * side - 2)], send_sem.at[0])
-        whole_wait(upd_send.at[pl.ds(0, 2 * side - 1)], send_sem.at[1])
+        whole_wait(prod_send.at[pl.ds(0, n - 2)], send_sem.at[0])
+        whole_wait(prod_send, send_sem.at[8])
+        whole_wait(upd_send.at[others], send_sem.at[1])
 
     whole_wait(prod_recv.at[others], send_sem.at[2])
     whole_wait(bias_recv.at[pl.ds(0, 2 * side - 1)], send_sem.at[3])
@@ -404,8 +440,6 @@
     whole_wait(o_recv.at[0], send_sem.at[5])
     whole_wait(o_recv.at[1], send_sem.at[6])
     whole_wait(upd_recv.at[:, others], send_sem.at[7])
-    whole_wait(edge_mid.at[pl.ds(0, side - 1)], send_sem.at[8])
-    whole_wait(pair_mid.at[pl.ds(0, side - 1)], send_sem.at[9])
     whole_wait(bias_recv.at[pl.ds(0, n - 2 * side)], send_sem.at[10])
 
 def local(n, *args):
@@ -449,6 +483,7 @@
             pltpu.SemaphoreType.DMA((side,)),
             pltpu.SemaphoreType.REGULAR,
             pltpu.SemaphoreType.REGULAR,
+            pltpu.SemaphoreType.REGULAR,
         ],
         compiler_params=pltpu.CompilerParams(collective_id=0, has_side_effects=True),
         name="pair_update",

time: 62 us -> 60.6 us (0.977)
  Pallas kernels: 61.2 us -> 59.8 us
    pallas_call x1, Pallas kernels: 61.2 us -> 59.8 us  [local(): pl.pallas_call(functools.partial(kernel, n), out_shape=pltpu.VMEM(args[0]...]
where the time goes in v7:
time: 60.6 us; the launch traced here: 60.5 us
  Pallas kernels  59.8 us (99%)
  local copies, waits for them, and re-layouts  0.66 us (1%)
    pallas_call x1, Pallas kernels, local(): pl.pallas_call(functools.partial(kernel, n), out_shape=pltpu.VMEM(args[0]...  59.8 us

profile of v7, /device:TPU:513, one launch (start us, length us, event | category | flops | bytes accessed | tf_op | source)
XLA Modules:
  0.0 60.5 jit_solution(17656284651919738381)
XLA Ops:
  0.0 59.8 %pair_update.1 = bf16[2,256,128]{2,1,0:T(8,128)(2,1)S(1)} custom-call(bf16[2,256,128]{2,1,0:T(8,128)(2,1)} %pair_hbm.1, s32[1,256]{1,0:T(1,128)} %bitcast.2, bf16[128,512]{1,0:T(8,128)(2,1)} %w_in_hbm.1, bf16[128,128]{1,0:T(8,128)(2,1)} %w_tg_hbm.1, bf16[128,128]{1,0:T(8,128)(2,1)} %w_to_hbm.1, bf16[128,384]{1,0:T(8,128)(2,1)} %w_qkv_hbm.1, ...), custom_call_target="tpu_custom_call" | custom-call | tf_op jit(solution)/shard_map/pair_update/pallas_call | solution.py:451
  59.8 0.7 %copy.11 = bf16[2,256,128]{2,1,0:T(8,128)(2,1)} copy(bf16[2,256,128]{2,1,0:T(8,128)(2,1)S(1)} %pair_update.1) | data formatting | bytes 262144

commit v8 on v7

--- a/solution.py
+++ b/solution.py
@@ -271,11 +271,10 @@
             pl.semaphore_wait(row_sem, side - 1)
             greet(0)
 
-        for low, high in spans[:2]:
-            second_leg(low, high, *edge_legs, True)
-
         @pl.when(feeds_first)
         def _():
+            for low, high in spans[:2]:
+                second_leg(low, high, *edge_legs, True)
             around_first(edge_send, edge_recv, 8, recv_sem.at[0])
             around_first(pair_send, pair_recv, 9, recv_sem.at[1])
             pl.semaphore_wait(late_sem, 1)
@@ -285,13 +284,13 @@
 
         @pl.when(jnp.logical_not(feeds_first))
         def _():
-            second_leg(*spans[2], *edge_legs, True)
+            for low, high in ((side // 2, side), (0, side // 2)):
+                second_leg(low, high, *edge_legs, True)
 
             @pl.when(ends_at_first)
             def _():
                 pl.semaphore_wait(late_sem, 1)
-                for low, high in spans:
-                    second_leg_late(low, high, edge_mid, edge_recv, 0, recv_sem.at[0])
+                second_leg_late(0, side, edge_mid, edge_recv, 0, recv_sem.at[0])
 
             second_leg(0, side, *pair_legs, False)
 
@@ -378,16 +377,18 @@
         pass_on(u)
     att_gates = [sigmoid(dot(att_own[jj], w_ag_ref[...])) for jj in range(2)]
 
+    ones = [jnp.broadcast_to(jnp.where(m, 1.0, 0.0), (res, cz)).astype(BF) for m in head_mask]
+    weighed = [[jnp.concatenate([jnp.where(head_mask[h], v, 0), ones[h]], axis=1) for h in range(2)] for v in values]
     whole_wait(bias_recv.at[pl.ds(0, n - 2 * side)], recv_sem.at[3])
     any_head = head_mask[0] | head_mask[1]
+    biases = [bias_recv[:, 2 * h : 2 * h + 2].reshape(res, res) for h in range(2)]
 
     def attended(l):
         total = None
         for h in range(2):
-            s = scores[2 * l + h] + bias_recv[:, 2 * h : 2 * h + 2].reshape(res, res)
+            s = scores[2 * l + h] + biases[h]
             e = jnp.exp(s - jnp.max(s, axis=1, keepdims=True)).astype(BF)
-            ones = jnp.broadcast_to(jnp.where(head_mask[h], 1.0, 0.0), (res, cz)).astype(BF)
-            part = dot(e, jnp.concatenate([jnp.where(head_mask[h], values[l], 0), ones], axis=1))
+            part = dot(e, weighed[l][h])
             total = part if total is None else total + part
         return (total[:, :cz] / jnp.where(any_head, total[:, cz:], 1.0)).astype(BF)
 

time: 60.6 us -> 60.4 us (level)
  no operation moved by 1% of the time
where the time goes in v8:
time: 60.4 us; the launch traced here: 60.3 us
  Pallas kernels  59.6 us (99%)
  local copies, waits for them, and re-layouts  0.66 us (1%)
    pallas_call x1, Pallas kernels, local(): pl.pallas_call(functools.partial(kernel, n), out_shape=pltpu.VMEM(args[0]...  59.6 us

profile of v8, /device:TPU:513, one launch (start us, length us, event | category | flops | bytes accessed | tf_op | source)
XLA Modules:
  0.0 60.3 jit_solution(9954664085114203702)
XLA Ops:
  0.0 59.6 %pair_update.1 = bf16[2,256,128]{2,1,0:T(8,128)(2,1)S(1)} custom-call(bf16[2,256,128]{2,1,0:T(8,128)(2,1)} %pair_hbm.1, s32[1,256]{1,0:T(1,128)} %bitcast.2, bf16[128,512]{1,0:T(8,128)(2,1)} %w_in_hbm.1, bf16[128,128]{1,0:T(8,128)(2,1)} %w_tg_hbm.1, bf16[128,128]{1,0:T(8,128)(2,1)} %w_to_hbm.1, bf16[128,384]{1,0:T(8,128)(2,1)} %w_qkv_hbm.1, ...), custom_call_target="tpu_custom_call" | custom-call | tf_op jit(solution)/shard_map/pair_update/pallas_call | solution.py:452
  59.6 0.7 %copy.11 = bf16[2,256,128]{2,1,0:T(8,128)(2,1)} copy(bf16[2,256,128]{2,1,0:T(8,128)(2,1)S(1)} %pair_update.1) | data formatting | bytes 262144
